TPU v7x, 32 devices: a whole 2x2x4 slice. The times are simulated.
32 devices in a mesh: dev: 32 (over z, y, x, core).
Axes of the slice: x: 2, y: 2, z: 4, core: 2. Of those that a mesh axis runs over, the one named last changes fastest.
Arguments:
- tokens: bfloat16 [576, 197, 384], P('dev'), may hold values from -6 to 6
- cotangent: bfloat16 [576, 197, 384], P('dev'), may hold values from -6 to 6
- valid_slots: int32 [576], P('dev'), may hold values from 0 to 1, as said below
- qkv_weight: bfloat16 [442368], P('dev'), may hold values from -0.3125 to 0.3125
- out_weight: bfloat16 [147456], P('dev'), may hold values from -1.25 to 1.25
- fc1_weight: bfloat16 [589824], P('dev'), may hold values from -0.3125 to 0.3125
- fc2_weight: bfloat16 [589824], P('dev'), may hold values from -0.15625 to 0.15625
- norm_params: bfloat16 [1536], P('dev'), may hold values from -2 to 2
- bias_params: bfloat16 [3072], P('dev'), may hold values from -3 to 3
Outputs:
- block_output: bfloat16 [576, 197, 384], P('dev')
- input_grad: float32 [576, 197, 384], P('dev')
- qkv_grad: float32 [442368], P('dev')
- out_grad: float32 [147456], P('dev')
- fc1_grad: float32 [589824], P('dev')
- fc2_grad: float32 [589824], P('dev')
- norm_grad: float32 [1536], P('dev')
- bias_grad: float32 [3072], P('dev')
Inputs may be any that keep to these rules, and one draw needn't show every extreme that they name: `valid_slots`: each device's 18 slots hold 18 or 17 images; in every draw some devices hold 18 and some 18 - 1.
All inputs are finite; a program needn't handle non-finite values.
Results may differ from a plain program's by a relative error of at most 0.011.
Values may be sent and summed in bfloat16 or wider, within the bound.
A program may use at most 320 MiB of HBM per device.

v0:
```python
import jax
import jax.numpy as jnp
from jax import lax
from jax.sharding import PartitionSpec as P

D = 384
HEADS = 6
HEAD_DIM = 64
FF = 1536


norm_eps = 1e-06


def normalize(value, gain, shift):
    mean = jnp.mean(value, axis=-1, keepdims=True)
    centered = value - mean
    inverse = lax.rsqrt(jnp.mean(centered * centered, axis=-1, keepdims=True) + norm_eps)
    normed = centered * inverse
    return (normed * gain + shift, normed, inverse)


def normalize_back(grad_out, normed, inverse, gain):
    scaled = grad_out * gain
    inner = jnp.mean(scaled, axis=-1, keepdims=True)
    along = jnp.mean(scaled * normed, axis=-1, keepdims=True)
    return inverse * (scaled - inner - normed * along)


def exact_gelu(value):
    return jax.nn.gelu(value, approximate=False)


def matmul(left, right):
    return jnp.dot(left, right, preferred_element_type=jnp.float32)


def across_rows(left, right):
    return lax.dot_general(
        left, right, (((0,), (0,)), ((), ())), preferred_element_type=jnp.float32
    )


def across_cols(left, right):
    return lax.dot_general(
        left, right, (((1,), (1,)), ((), ())), preferred_element_type=jnp.float32
    )


def local(
    tokens,
    cotangent,
    valid_slots,
    qkv_weight,
    out_weight,
    fc1_weight,
    fc2_weight,
    norm_params,
    bias_params,
):
    images = tokens.shape[0]
    length = tokens.shape[1]
    rows_total = images * length
    scale = HEAD_DIM ** (-0.5)
    head_shape = (images, length, HEADS, HEAD_DIM)
    attn_whole = (
        lax.all_gather(qkv_weight, "dev", axis=0, tiled=True),
        lax.all_gather(out_weight, "dev", axis=0, tiled=True),
        lax.all_gather(norm_params, "dev", axis=0, tiled=True),
        lax.all_gather(bias_params, "dev", axis=0, tiled=True),
    )
    qkv_full = attn_whole[0].reshape(D, 3 * D)
    out_full = attn_whole[1].reshape(D, D)
    norm_full = attn_whole[2].astype(jnp.float32)
    bias_full = attn_whole[3].astype(jnp.float32)
    gain_one = norm_full[:D]
    shift_one = norm_full[D : 2 * D]
    gain_two = norm_full[2 * D : 3 * D]
    shift_two = norm_full[3 * D :]
    bias_query = bias_full[:D]
    bias_value = bias_full[D : 2 * D]
    bias_attn = bias_full[2 * D : 3 * D]
    bias_hidden = bias_full[3 * D : 3 * D + FF]
    bias_mlp = bias_full[3 * D + FF :]
    inputs = tokens.astype(jnp.float32).reshape(rows_total, D)
    normed_one, unit_one, inverse_one = normalize(inputs, gain_one, shift_one)
    low_one = normed_one.astype(jnp.bfloat16)
    projected = matmul(low_one, qkv_full)
    queries = (projected[:, :D] + bias_query).astype(jnp.bfloat16).reshape(head_shape)
    keys_low = projected[:, D : 2 * D].astype(jnp.bfloat16).reshape(head_shape)
    values_low = (projected[:, 2 * D :] + bias_value).astype(jnp.bfloat16).reshape(head_shape)
    scores = (
        jnp.einsum("bqhd,bkhd->bhqk", queries, keys_low, preferred_element_type=jnp.float32) * scale
    )
    top_score = jnp.max(scores, axis=-1, keepdims=True)
    log_total = top_score + jnp.log(jnp.sum(jnp.exp(scores - top_score), axis=-1, keepdims=True))
    weights_low = jnp.exp(scores - log_total).astype(jnp.bfloat16)
    mixed = jnp.einsum(
        "bhqk,bkhd->bqhd", weights_low, values_low, preferred_element_type=jnp.float32
    )
    mixed_low = mixed.reshape(rows_total, D).astype(jnp.bfloat16)
    residual = inputs + matmul(mixed_low, out_full) + bias_attn
    ff_whole = (
        lax.all_gather(fc1_weight, "dev", axis=0, tiled=True),
        lax.all_gather(fc2_weight, "dev", axis=0, tiled=True),
    )
    fc1_full = ff_whole[0].reshape(D, FF)
    fc2_full = ff_whole[1].reshape(FF, D)
    normed_two, unit_two, inverse_two = normalize(residual, gain_two, shift_two)
    low_two = normed_two.astype(jnp.bfloat16)
    hidden_pre = matmul(low_two, fc1_full) + bias_hidden
    hidden_low = exact_gelu(hidden_pre).astype(jnp.bfloat16)
    result = residual + matmul(hidden_low, fc2_full) + bias_mlp
    row_mask = jnp.repeat(valid_slots.astype(jnp.float32), length)[:, None]
    outputs = (result * row_mask).reshape(images, length, D).astype(jnp.bfloat16)
    ff_again = (
        lax.all_gather(fc1_weight, "dev", axis=0, tiled=True),
        lax.all_gather(fc2_weight, "dev", axis=0, tiled=True),
        lax.all_gather(norm_params, "dev", axis=0, tiled=True),
    )
    fc1_back = ff_again[0].reshape(D, FF)
    fc2_back = ff_again[1].reshape(FF, D)
    norm_again = ff_again[2].astype(jnp.float32)
    gain_one_back = norm_again[:D]
    gain_two_back = norm_again[2 * D : 3 * D]
    grad_result = cotangent.astype(jnp.float32).reshape(rows_total, D) * row_mask
    grad_bias_mlp = jnp.sum(grad_result, axis=0)
    grad_mlp_low = grad_result.astype(jnp.bfloat16)
    grad_fc2 = across_rows(hidden_low, grad_mlp_low)
    grad_hidden = across_cols(grad_mlp_low, fc2_back)
    _, gelu_pull = jax.vjp(exact_gelu, hidden_pre)
    grad_pre = gelu_pull(grad_hidden)[0]
    grad_bias_hidden = jnp.sum(grad_pre, axis=0)
    grad_pre_low = grad_pre.astype(jnp.bfloat16)
    grad_fc1 = across_rows(low_two, grad_pre_low)
    grad_normed_two = across_cols(grad_pre_low, fc1_back)
    grad_gain_two = jnp.sum(grad_normed_two * unit_two, axis=0)
    grad_shift_two = jnp.sum(grad_normed_two, axis=0)
    grad_residual = grad_result + normalize_back(
        grad_normed_two, unit_two, inverse_two, gain_two_back
    )
    ff_shards = (
        lax.psum_scatter(grad_fc1.reshape(-1), "dev", scatter_dimension=0, tiled=True),
        lax.psum_scatter(grad_fc2.reshape(-1), "dev", scatter_dimension=0, tiled=True),
    )
    attn_again = (
        lax.all_gather(qkv_weight, "dev", axis=0, tiled=True),
        lax.all_gather(out_weight, "dev", axis=0, tiled=True),
    )
    qkv_back = attn_again[0].reshape(D, 3 * D)
    out_back = attn_again[1].reshape(D, D)
    grad_bias_attn = jnp.sum(grad_residual, axis=0)
    grad_attn_low = grad_residual.astype(jnp.bfloat16)
    grad_out = across_rows(mixed_low, grad_attn_low)
    grad_mixed = across_cols(grad_attn_low, out_back).astype(jnp.bfloat16).reshape(head_shape)
    scores_again = (
        jnp.einsum("bqhd,bkhd->bhqk", queries, keys_low, preferred_element_type=jnp.float32) * scale
    )
    weights_again = jnp.exp(scores_again - log_total)
    weights_again_low = weights_again.astype(jnp.bfloat16)
    grad_values = jnp.einsum(
        "bhqk,bqhd->bkhd", weights_again_low, grad_mixed, preferred_element_type=jnp.float32
    )
    grad_weights = jnp.einsum(
        "bqhd,bkhd->bhqk", grad_mixed, values_low, preferred_element_type=jnp.float32
    )
    grad_scores = weights_again * (
        grad_weights - jnp.sum(grad_weights * weights_again, axis=-1, keepdims=True)
    )
    grad_scores_low = grad_scores.astype(jnp.bfloat16)
    grad_queries = (
        jnp.einsum("bhqk,bkhd->bqhd", grad_scores_low, keys_low, preferred_element_type=jnp.float32)
        * scale
    )
    grad_keys = (
        jnp.einsum("bhqk,bqhd->bkhd", grad_scores_low, queries, preferred_element_type=jnp.float32)
        * scale
    )
    grad_queries = grad_queries.reshape(rows_total, D)
    grad_keys = grad_keys.reshape(rows_total, D)
    grad_values = grad_values.reshape(rows_total, D)
    grad_bias_query = jnp.sum(grad_queries, axis=0)
    grad_bias_value = jnp.sum(grad_values, axis=0)
    grad_projected = jnp.concatenate([grad_queries, grad_keys, grad_values], axis=1).astype(
        jnp.bfloat16
    )
    grad_qkv = across_rows(low_one, grad_projected)
    grad_normed_one = across_cols(grad_projected, qkv_back)
    grad_gain_one = jnp.sum(grad_normed_one * unit_one, axis=0)
    grad_shift_one = jnp.sum(grad_normed_one, axis=0)
    grad_inputs = grad_residual + normalize_back(
        grad_normed_one, unit_one, inverse_one, gain_one_back
    )
    grad_norm = jnp.concatenate([grad_gain_one, grad_shift_one, grad_gain_two, grad_shift_two])
    grad_bias = jnp.concatenate(
        [grad_bias_query, grad_bias_value, grad_bias_attn, grad_bias_hidden, grad_bias_mlp]
    )
    attn_shards = (
        lax.psum_scatter(grad_qkv.reshape(-1), "dev", scatter_dimension=0, tiled=True),
        lax.psum_scatter(grad_out.reshape(-1), "dev", scatter_dimension=0, tiled=True),
        lax.psum_scatter(grad_norm, "dev", scatter_dimension=0, tiled=True),
        lax.psum_scatter(grad_bias, "dev", scatter_dimension=0, tiled=True),
    )
    shards = (
        attn_shards[0],
        attn_shards[1],
        ff_shards[0],
        ff_shards[1],
        attn_shards[2],
        attn_shards[3],
    )
    return (
        outputs,
        grad_inputs.reshape(images, length, D),
        shards[0],
        shards[1],
        shards[2],
        shards[3],
        shards[4],
        shards[5],
    )


def solution(mesh):
    return jax.shard_map(
        local,
        mesh=mesh,
        in_specs=(
            P("dev", None, None),
            P("dev", None, None),
            P("dev"),
            P("dev"),
            P("dev"),
            P("dev"),
            P("dev"),
            P("dev"),
            P("dev"),
        ),
        out_specs=(
            P("dev", None, None),
            P("dev", None, None),
            P("dev"),
            P("dev"),
            P("dev"),
            P("dev"),
            P("dev"),
            P("dev"),
        ),
        check_vma=False,
    )
```

profile of v0, /device:TPU:0, one launch (start us, length us, event | category | flops | bytes accessed | tf_op | source)
XLA Modules:
  0.0 761.2 jit_solution(12885175933710942524)
XLA Ops:
  8.7 2.6 convert_reduce_fusion
  11.4 4.0 reshape.196
  15.9 42.2 %all-reduce.10 = (bf16[1536]{0:T(1024)(128)(2,1)S(1)}, bf16[3072]{0:T(1024)(128)(2,1)S(1)}) all-reduce(bf16[1536]{0:T(1024)(128)(2,1)S(1)} %dynamic-update-slice, bf16[3072]{0:T(1024)(128)(2,1)S(1)} %dynamic-update-slice.1), channel_id=1, replica_groups=mesh['dev'=32] {'dev'}, use_global_device_ids=true, to_apply=%add | all-reduce | flops 4608 | bytes 18432
  62.8 2.4 add_convert_fusion
  65.1 3.7 convert_element_type.82
  68.9 45.9 %all-gather = bf16[32,1,13824]{2,1,0:T(2,128)(2,1)S(1)} all-gather(bf16[1,1,13824]{2,1,0:T(2,128)(2,1)S(1)} %reshape.218), channel_id=1, replica_groups=mesh['dev'=32] {'dev'}, dimensions={0}, use_global_device_ids=true | all-gather | bytes 912384 | tf_op jit(solution)/shard_map/all_gather | solution.py:67
  114.7 5.3 reduce.5
  121.4 7.4 fusion.37
  130.8 3.4 fusion.8
  134.2 9.3 %reshape.225 = bf16[18,197,6,64]{3,2,1,0:T(8,128)(2,1)} reshape(bf16[3546,384]{1,0:T(8,128)(2,1)} %get-tuple-element.28) | data formatting | bytes 5446656 | tf_op jit(solution)/shard_map/reshape | solution.py:89
  143.5 9.2 %copy.52 = bf16[18,197,6,64]{1,3,2,0:T(8,128)(2,1)} copy(bf16[18,197,6,64]{3,2,1,0:T(8,128)(2,1)} %reshape.225) | data formatting | bytes 5446656 | tf_op jit(solution)/shard_map/reshape | solution.py:89
  152.7 6.7 reshape.226
  159.3 7.6 %copy.53 = bf16[18,197,6,64]{1,3,2,0:T(8,128)(2,1)S(1)} copy(bf16[18,197,6,64]{3,2,1,0:T(8,128)(2,1)} %reshape.226) | data formatting | bytes 5446656 | tf_op jit(solution)/shard_map/reshape | solution.py:90
  167.0 13.8 %multiply_reduce_fusion.1 = (f32[18,6,197]{2,1,0:T(8,128)S(1)}, f32[18,6,197,197]{2,3,1,0:T(8,128)}) fusion(bf16[18,197,6,64]{1,3,2,0:T(8,128)(2,1)} %copy.52, bf16[18,197,6,64]{1,3,2,0:T(8,128)(2,1)S(1)} %copy.53), kind=kOutput, calls=%fused_computation.21 | convolution fusion | flops 544857088 | bytes 22297248 | tf_op jit(solution)/shard_map/bqhd,bkhd->bhqk/dot_general | solution.py:93
  180.8 11.4 %exponential_reduce_fusion = f32[18,6,197]{2,1,0:T(8,128)S(1)} fusion(f32[18,6,197,197]{2,3,1,0:T(8,128)} %get-tuple-element.41, f32[18,6,197]{2,1,0:T(8,128)S(1)} %get-tuple-element.40), kind=kLoop, calls=%fused_computation.4 | loop fusion | flops 12552840 | bytes 16935696 | tf_op jit(solution)/shard_map/reduce_sum | solution.py:96
  192.9 6.7 reshape.224
  199.6 7.6 %copy.54 = bf16[18,197,6,64]{1,3,2,0:T(8,128)(2,1)S(1)} copy(bf16[18,197,6,64]{3,2,1,0:T(8,128)(2,1)} %reshape.224) | data formatting | bytes 5446656 | tf_op jit(solution)/shard_map/reshape | solution.py:91
  207.2 14.7 %convert_bitcast_fusion = bf16[18,197,6,64]{1,3,2,0:T(8,128)(2,1)} fusion(bf16[18,197,6,64]{1,3,2,0:T(8,128)(2,1)S(1)} %copy.54, f32[18,6,197,197]{2,3,1,0:T(8,128)} %get-tuple-element.41, f32[18,6,197]{2,1,0:T(8,128)} %log_add_fusion), kind=kOutput, calls=%fused_computation.62 | convolution fusion | flops 550431424 | bytes 22297248 | tf_op jit(solution)/shard_map/bhqk,bkhd->bqhd/dot_general | solution.py:98
  221.9 6.4 copy.56
  228.3 6.5 convert_element_type.89
  234.9 38.5 %all-gather.1 = bf16[32,1,4608]{2,1,0:T(2,128)(2,1)S(1)} all-gather(bf16[1,1,4608]{2,1,0:T(2,128)(2,1)S(1)} %reshape.220), channel_id=1, replica_groups=mesh['dev'=32] {'dev'}, dimensions={0}, use_global_device_ids=true | all-gather | bytes 304128 | tf_op jit(solution)/shard_map/all_gather | solution.py:68
  273.3 2.4 reduce.6
  277.1 4.7 fusion.35
  281.9 2.7 copy-done.2
  284.6 2.1 multiply_reduce_fusion.7
  286.8 3.1 reshape.204
  290.0 3.2 multiply_reduce_fusion.8
  293.2 3.7 convert_element_type.97
  297.6 2.7 reshape.202
  300.4 55.8 %multiply_convert_fusion.1 = (bf16[3546,1536]{1,0:T(8,128)(2,1)}, f32[3546,1536]{1,0:T(8,128)}, f32[3546,1536]{1,0:T(8,128)}) fusion(f32[1536]{0:T(1024)S(1)} %copy-done.43, bf16[384,1536]{1,0:T(8,128)(2,1)S(1)} %reshape.202, f32[3546,384]{1,0:T(8,128)} %copy-done.2, f32[384]{0:T(512)S(1)} %copy-done.45, f32[384]{0:T(512)S(1)} %copy-done.41, ...), kind=kOutput, calls=%fused_computation.7 | convolution fusion | flops 4549319680 | bytes 61130448 | tf_op jit(solution)/shard_map/dot_general | solution.py:35
  356.3 2.4 reshape.203
  358.7 26.8 %fusion.36 = (f32[1536]{0:T(1024)}, bf16[3546,1536]{1,0:T(8,128)(2,1)}) fusion(f32[3546,1536]{1,0:T(8,128)} %get-tuple-element.27, bf16[3546,384]{1,0:T(8,128)(2,1)} %convert_element_type.97, bf16[1536,384]{1,0:T(8,128)(2,1)S(1)} %reshape.203, f32[3546,1536]{1,0:T(8,128)} %get-tuple-element.44, f32[1536]{0:T(1024)S(1)} %copy-done.43), kind=kOutput, calls=%fused_computation.99 | convolution fusion | flops 4270176768 | bytes 58381824 | tf_op jit(solution)/shard_map/dot_general | solution.py:45
  385.5 11.3 %multiply_reduce_fusion.3 = (f32[384]{0:T(512)}, f32[3546]{0:T(1024)S(1)}, f32[3546]{0:T(1024)S(1)}, f32[384]{0:T(512)}, f32[3546,384]{1,0:T(8,128)S(1)}) fusion(f32[3546,384]{1,0:T(8,128)S(1)} %bitcast.50, f32[3546]{0:T(1024)S(1)} %add_rsqrt_fusion.1, f32[3546]{0:T(1024)S(1)} %broadcast_multiply_fusion.5, f32[384]{0:T(512)S(1)} %copy-done.41, ...), kind=kOutput, calls=%fused_computation.39 | convolution fusion | flops 4195278848 | bytes 23027616 | tf_op jit(solution)/shard_map/dot_general | solution.py:45
  396.8 4.0 fusion.31
  400.7 2.4 copy-done.1
  405.0 6.7 reshape.227
  411.7 7.6 %copy.58 = bf16[18,197,6,64]{1,3,2,0:T(8,128)(2,1)S(1)} copy(bf16[18,197,6,64]{3,2,1,0:T(8,128)(2,1)} %reshape.227) | data formatting | bytes 5446656 | tf_op jit(solution)/shard_map/reshape | solution.py:155
  419.3 11.9 %bitcast_convert_fusion = (bf16[18,197,6,64]{1,3,2,0:T(8,128)(2,1)}, f32[18,6,64,197]{3,2,1,0:T(8,128)}) fusion(bf16[18,197,6,64]{1,3,2,0:T(8,128)(2,1)S(1)} %copy.58, f32[18,6,197,197]{2,3,1,0:T(8,128)} %get-tuple-element.41, f32[18,6,197]{2,1,0:T(8,128)} %log_add_fusion), kind=kOutput, calls=%fused_computation.24 | convolution fusion | flops 550431424 | bytes 27743904 | tf_op jit(solution)/shard_map/bhqk,bqhd->bkhd/dot_general | solution.py:161
  431.1 17.4 %multiply_reduce_fusion = (f32[18,6,197]{2,1,0:T(8,128)}, f32[18,6,197,197]{2,3,1,0:T(8,128)}) fusion(f32[18,6,197,197]{2,3,1,0:T(8,128)} %get-tuple-element.41, f32[18,6,197]{2,1,0:T(8,128)} %log_add_fusion, bf16[18,197,6,64]{1,3,2,0:T(8,128)(2,1)S(1)} %copy.58, bf16[18,197,6,64]{1,3,2,0:T(8,128)(2,1)} %copy-done.9), kind=kOutput, calls=%fused_computation.2 | convolution fusion | flops 553239808 | bytes 39147840 | tf_op jit(solution)/shard_map/bqhd,bkhd->bhqk/dot_general | solution.py:164
  448.6 15.2 %multiply_convert_fusion = bf16[18,6,197,197]{2,3,1,0:T(8,128)(2,1)S(1)} fusion(f32[18,6,197,197]{2,3,1,0:T(8,128)} %get-tuple-element.47, f32[18,6,197,197]{2,3,1,0:T(8,128)} %get-tuple-element.41, f32[18,6,197]{2,1,0:T(8,128)} %get-tuple-element.46, f32[18,6,197]{2,1,0:T(8,128)} %log_add_fusion), kind=kLoop, calls=%fused_computation.1 | loop fusion | flops 20956860 | bytes 42083928 | tf_op jit(solution)/shard_map/convert_element_type | solution.py:170
  463.8 4.2 copy-done
  468.0 6.2 bitcast_convert_fusion.1
  474.2 9.5 %fusion.14 = bf16[18,197,6,64]{1,3,2,0:T(8,128)(2,1)} fusion(bf16[18,197,6,64]{1,3,2,0:T(8,128)(2,1)S(1)} %copy-done.8, bf16[18,6,197,197]{2,3,1,0:T(8,128)(2,1)} %copy-done), kind=kOutput, calls=%fused_computation.61 | convolution fusion | flops 539218944 | bytes 13829400 | tf_op jit(solution)/shard_map/bhqk,bqhd->bkhd/dot_general | solution.py:176
  483.7 11.9 %fusion.10 = f32[384,1536]{1,0:T(8,128)} fusion(bf16[3546,1536]{1,0:T(8,128)(2,1)} %get-tuple-element.54, f32[3546,384]{1,0:T(8,128)} %copy-done.2, f32[384]{0:T(512)} %get-tuple-element.37, f32[384]{0:T(512)} %get-tuple-element.36, f32[3546]{0:T(1024)} %copy-done.29, f32[3546]{0:T(1024)S(1)} %broadcast_multiply_fusion.5), kind=kOutput, calls=%fused_computation.47 | convolution fusion | flops 4189840128 | bytes 18730704 | tf_op jit(solution)/shard_map/dot_general | solution.py:39
  495.6 4.6 copy.68
  500.2 8.2 %reshape.208 = bf16[3546,384]{0,1:T(8,128)(2,1)} reshape(bf16[18,197,6,64]{1,0,3,2:T(8,128)(2,1)} %copy.68) | data formatting | bytes 5446656 | tf_op jit(solution)/shard_map/reshape | solution.py:181
  508.4 4.5 copy.65
  513.0 7.8 %reshape.207 = bf16[3546,384]{0,1:T(8,128)(2,1)} reshape(bf16[18,197,6,64]{1,0,3,2:T(8,128)(2,1)} %copy.65) | data formatting | bytes 5446656 | tf_op jit(solution)/shard_map/reshape | solution.py:180
  520.8 4.5 copy.62
  525.3 7.8 %reshape.206 = bf16[3546,384]{0,1:T(8,128)(2,1)} reshape(bf16[18,197,6,64]{1,0,3,2:T(8,128)(2,1)} %copy.62) | data formatting | bytes 5446656 | tf_op jit(solution)/shard_map/reshape | solution.py:179
  533.2 2.1 constant_dynamic-update-slice_fusion.2
  536.0 4.2 copy-done.26
  540.2 10.0 %multiply_reduce_fusion.4 = (f32[384]{0:T(512)S(1)}, f32[3546]{0:T(1024)S(1)}, f32[3546]{0:T(1024)S(1)}, f32[384]{0:T(512)S(1)}, f32[3546,384]{1,0:T(8,128)}) fusion(f32[3546,384]{1,0:T(8,128)S(1)} %bitcast.52, f32[3546]{0:T(1024)S(1)} %copy-done.30, f32[3546]{0:T(1024)S(1)} %copy-done.31, f32[384]{0:T(512)S(1)} %copy-done.34, ...), kind=kOutput, calls=%fused_computation.40 | convolution fusion | flops 3149520896 | bytes 20009376 | tf_op jit(solution)/shard_map/dot_general | solution.py:45
  550.3 9.7 %fusion.16 = f32[384,1152]{1,0:T(8,128)} fusion(bf16[3546,1152]{0,1:T(8,128)(2,1)} %copy-done.26, f32[3546,384]{1,0:T(8,128)S(1)} %bitcast.52, f32[384]{0:T(512)S(1)} %copy-done.40, f32[3546]{0:T(1024)S(1)} %copy-done.30, f32[384]{0:T(512)S(1)} %copy-done.34, f32[3546]{0:T(1024)S(1)} %copy-done.31), kind=kOutput, calls=%fused_computation.64 | convolution fusion | flops 3144082176 | bytes 15417552 | tf_op jit(solution)/shard_map/dot_general | solution.py:39
  561.6 3.6 bitcast_reduce_fusion
  565.3 3.7 bitcast_reduce_fusion.1
  570.6 2.5 reshape.210
  574.0 10.4 %fusion.15 = f32[1536,384]{1,0:T(8,128)S(1)} fusion(bf16[3546,1536]{1,0:T(8,128)(2,1)} %get-tuple-element.26, f32[3546,384]{1,0:T(8,128)} %reshape.204, f32[3546]{0:T(1024)S(1)} %copy-done.28), kind=kOutput, calls=%fused_computation.63 | convolution fusion | flops 4185755136 | bytes 18713448 | tf_op jit(solution)/shard_map/dot_general | solution.py:39
  586.0 9.3 %multiply_add_fusion.1 = f32[3546,384]{1,0:T(8,128)} fusion(f32[3546,384]{1,0:T(8,128)} %copy-done.1, f32[3546,384]{1,0:T(8,128)} %get-tuple-element.52, f32[3546,384]{1,0:T(8,128)} %reshape.196, f32[3546]{0:T(1024)S(1)} %broadcast_multiply_fusion.1, f32[3546]{0:T(1024)S(1)} %copy-done.30, f32[3546]{0:T(1024)S(1)} %broadcast_multiply_fusion.2, ...), kind=kLoop, calls=%fused_computation.42 | loop fusion | flops 10893312 | bytes 21844896 | tf_op jit(solution)/shard_map/add | solution.py:191
  595.3 4.6 reshape.209
  600.0 10.5 %multiply_convert_fusion.3 = bf16[3546,384]{1,0:T(8,128)(2,1)S(1)} fusion(f32[3546,384]{1,0:T(8,128)} %copy-done.2, bf16[3546,1536]{1,0:T(8,128)(2,1)} %get-tuple-element.26, bf16[1536,384]{1,0:T(8,128)(2,1)} %copy-done.24, f32[3546]{0:T(1024)S(1)} %copy-done.28, f32[384]{0:T(512)S(1)} %copy-done.44), kind=kOutput, calls=%fused_computation.51 | convolution fusion | flops 4188478464 | bytes 20258664 | tf_op jit(solution)/shard_map/dot_general | solution.py:35
  610.6 2.2 convert_element_type.94
  612.9 37.9 %all-reduce.8 = (f32[1536]{0:T(1024)S(1)}, f32[3072]{0:T(1024)S(1)}) all-reduce(f32[1536]{0:T(1024)S(1)} %pad_maximum_fusion, f32[3072]{0:T(1024)S(1)} %constant_dynamic-update-slice_fusion.6), channel_id=6, replica_groups=mesh['dev'=32] {'dev'}, use_global_device_ids=true, to_apply=%region_19.0.clone | all-reduce | flops 4608 | bytes 36864
  652.0 96.5 %all-reduce.13.cloned.1.call-done = (f32[442368]{0:T(1024)}, f32[147456]{0:T(1024)}, f32[589824]{0:T(1024)}, f32[589824]{0:T(1024)}) async-done(((f32[442368]{0:T(1024)}, f32[147456]{0:T(1024)}, f32[589824]{0:T(1024)}, f32[589824]{0:T(1024)}), (f32[442368]{0:T(1024)}, f32[147456]{0:T(1024)}, f32[589824]{0:T(1024)}, f32[589824]{0:T(1024)})) %all-reduce.13.cloned.1.call-update) | async-done | bytes 7077904
  (169 shorter events, 28.5 us)
Async XLA Ops:
  7.2 290.4 %all-gather.5.cloned.1.call-start = ((), (), s32[]{:S(2)}) async-start(), calls=%async_computation | async-start | bytes 1216512 | tf_op jit(solution)/shard_map/all_gather | solution.py:104
  7.9 348.3 %all-gather.7.cloned.1.call-start = ((), (), s32[]{:S(2)}) async-start(), calls=%async_computation.1 | async-start | bytes 1216512 | tf_op jit(solution)/shard_map/all_gather | solution.py:105
  8.7 739.8 %all-reduce.13.cloned.1.call-start = ((), (), s32[]{:S(2)}) async-start(), calls=%async_computation.2 | async-start | bytes 14155776
  8.7 6.7 copy-start.48
  8.7 6.9 copy-start.49
  8.7 50.5 %copy-start.5 = (bf16[18,197,384]{2,1,0:T(8,128)(2,1)S(1)}, bf16[18,197,384]{2,1,0:T(8,128)(2,1)}, u32[]{:S(2)}) copy-start(bf16[18,197,384]{2,1,0:T(8,128)(2,1)} %param.9) | copy-start | bytes 8169988
  62.0 6.8 copy-start.33
  62.0 6.8 copy-start.39
  62.8 6.0 copy-start.32
  121.4 7.4 copy-start.19
  143.5 9.2 %copy-start.17 = (bf16[3546,384]{1,0:T(8,128)(2,1)S(1)}, bf16[3546,384]{1,0:T(8,128)(2,1)}, u32[]{:S(2)}) copy-start(bf16[3546,384]{1,0:T(8,128)(2,1)} %slice.70) | copy-start | bytes 8169988
  166.9 13.8 %copy-start.3 = (bf16[18,197,6,64]{1,3,2,0:T(8,128)(2,1)}, bf16[18,197,6,64]{1,3,2,0:T(8,128)(2,1)S(1)}, u32[]{:S(2)}) copy-start(bf16[18,197,6,64]{1,3,2,0:T(8,128)(2,1)S(1)} %copy.53) | copy-start | bytes 8169988
  180.8 12.1 %copy-start.18 = (bf16[3546,384]{1,0:T(8,128)(2,1)S(1)}, bf16[3546,384]{1,0:T(8,128)(2,1)}, u32[]{:S(2)}) copy-start(bf16[3546,384]{1,0:T(8,128)(2,1)} %get-tuple-element.29) | copy-start | bytes 8169988
  207.2 14.8 %copy-start.9 = (bf16[18,197,6,64]{1,3,2,0:T(8,128)(2,1)}, bf16[18,197,6,64]{1,3,2,0:T(8,128)(2,1)S(1)}, u32[]{:S(2)}) copy-start(bf16[18,197,6,64]{1,3,2,0:T(8,128)(2,1)S(1)} %copy.54) | copy-start | bytes 8169988
  228.3 6.5 copy-start.36
  234.8 47.0 %copy-start.6 = (bf16[3546,384]{0,1:T(8,128)(2,1)}, bf16[3546,384]{0,1:T(8,128)(2,1)S(1)}, u32[]{:S(2)}) copy-start(bf16[3546,384]{0,1:T(8,128)(2,1)S(1)} %convert_element_type.89) | copy-start | bytes 8169988
  277.1 4.7 copy-start.21
  281.8 2.8 copy-start.2
  281.8 4.9 copy-start.50
  281.9 4.9 copy-start.14
  286.8 110.0 %copy-start.29 = (f32[3546]{0:T(1024)}, f32[3546]{0:T(1024)S(1)}, u32[]{:S(2)}) copy-start(f32[3546]{0:T(1024)S(1)} %add_rsqrt_fusion.1) | copy-start | bytes 42556
  290.0 10.4 %copy-start.41 = (f32[384]{0:T(512)S(1)}, f32[384]{0:T(512)}, u32[]{:S(2)}) copy-start(f32[384]{0:T(512)} %get-tuple-element.36) | copy-start | bytes 4612
  290.0 10.4 %copy-start.43 = (f32[1536]{0:T(1024)S(1)}, f32[1536]{0:T(1024)}, u32[]{:S(2)}) copy-start(f32[1536]{0:T(1024)} %slice.61) | copy-start | bytes 18436
  290.0 10.4 %copy-start.45 = (f32[384]{0:T(512)S(1)}, f32[384]{0:T(512)}, u32[]{:S(2)}) copy-start(f32[384]{0:T(512)} %get-tuple-element.37) | copy-start | bytes 4612
  300.3 55.9 %copy-start.25 = (bf16[384,1536]{1,0:T(8,128)(2,1)}, bf16[384,1536]{1,0:T(8,128)(2,1)S(1)}, u32[]{:S(2)}) copy-start(bf16[384,1536]{1,0:T(8,128)(2,1)S(1)} %reshape.202) | copy-start | bytes 3538948
  356.2 29.2 %slice-start.2 = ((s8[5455872]{0:T(1024)(128)(4,1)}), s8[1261568]{0:T(1024)(128)(4,1)S(1)}, s32[]{:S(2)}) async-start(s8[5455872]{0:T(1024)(128)(4,1)} %bitcast.49), calls=%async_computation.5 | async-start | bytes 2523136
  358.7 26.8 %copy-start.24 = (bf16[1536,384]{1,0:T(8,128)(2,1)}, bf16[1536,384]{1,0:T(8,128)(2,1)S(1)}, u32[]{:S(2)}) copy-start(bf16[1536,384]{1,0:T(8,128)(2,1)S(1)} %reshape.203) | copy-start | bytes 3538948
  358.7 26.8 %slice-start.3 = ((s8[5455872]{0:T(1024)(128)(4,1)}), s8[4194304]{0:T(1024)(128)(4,1)S(1)}, s32[]{:S(2)}) async-start(s8[5455872]{0:T(1024)(128)(4,1)} %bitcast.49), calls=%async_computation.6 | async-start | bytes 8388608
  385.5 11.3 %copy-start.11 = (f32[3546,384]{1,0:T(8,128)S(1)}, f32[3546,384]{1,0:T(8,128)}, u32[]{:S(2)}) copy-start(f32[3546,384]{1,0:T(8,128)} %reshape.204) | copy-start | bytes 16339972
  385.5 11.3 %copy-start.27 = (f32[3546]{0:T(1024)S(1)}, f32[3546]{0:T(1024)}, u32[]{:S(2)}) copy-start(f32[3546]{0:T(1024)} %mul.191) | copy-start | bytes 42556
  396.8 6.4 copy-start.22
  400.7 2.4 copy-start.1
  448.6 19.4 %copy-start.4 = (bf16[18,197,6,64]{1,3,2,0:T(8,128)(2,1)S(1)}, bf16[18,197,6,64]{1,3,2,0:T(8,128)(2,1)}, u32[]{:S(2)}) copy-start(bf16[18,197,6,64]{1,3,2,0:T(8,128)(2,1)} %copy-done.3) | copy-start | bytes 8169988
  463.8 4.2 copy-start
  468.0 6.2 copy-start.8
  483.7 11.9 %copy-start.12 = (bf16[18,197,6,64]{1,3,2,0:T(8,128)(2,1)S(1)}, bf16[18,197,6,64]{1,3,2,0:T(8,128)(2,1)}, u32[]{:S(2)}) copy-start(bf16[18,197,6,64]{1,3,2,0:T(8,128)(2,1)} %get-tuple-element.50) | copy-start | bytes 8169988
  500.2 8.2 %copy-start.13 = (bf16[18,197,6,64]{1,3,2,0:T(8,128)(2,1)S(1)}, bf16[18,197,6,64]{1,3,2,0:T(8,128)(2,1)}, u32[]{:S(2)}) copy-start(bf16[18,197,6,64]{1,3,2,0:T(8,128)(2,1)} %fusion.14) | copy-start | bytes 8169988
  513.0 7.8 %copy-start.10 = (bf16[18,197,6,64]{1,3,2,0:T(8,128)(2,1)S(1)}, bf16[18,197,6,64]{1,3,2,0:T(8,128)(2,1)}, u32[]{:S(2)}) copy-start(bf16[18,197,6,64]{1,3,2,0:T(8,128)(2,1)} %get-tuple-element.48) | copy-start | bytes 8169988
  525.3 9.9 %copy-start.16 = (bf16[3546,384]{0,1:T(8,128)(2,1)S(1)}, bf16[3546,384]{0,1:T(8,128)(2,1)}, u32[]{:S(2)}) copy-start(bf16[3546,384]{0,1:T(8,128)(2,1)} %reshape.207) | copy-start | bytes 8169988
  533.2 2.6 copy-start.15
  533.2 7.0 slice-start.4
  535.3 4.9 slice-start.5
  535.3 4.9 copy-start.20
  535.3 4.8 copy-start.30
  535.3 4.8 copy-start.31
  535.3 4.8 copy-start.34
  535.8 24.2 %slice-start = ((s8[5455872]{0:T(1024)(128)(4,1)}), s8[4194304]{0:T(1024)(128)(4,1)S(1)}, s32[]{:S(2)}) async-start(s8[5455872]{0:T(1024)(128)(4,1)} %bitcast.47), calls=%async_computation.3 | async-start | bytes 8388608
  535.9 4.2 copy-start.26
  540.2 10.1 %copy-start.40 = (f32[384]{0:T(512)S(1)}, f32[384]{0:T(512)}, u32[]{:S(2)}) copy-start(f32[384]{0:T(512)} %copy-done.39) | copy-start | bytes 4612
  540.2 19.8 %slice-start.1 = ((s8[5455872]{0:T(1024)(128)(4,1)}), s8[1261568]{0:T(1024)(128)(4,1)S(1)}, s32[]{:S(2)}) async-start(s8[5455872]{0:T(1024)(128)(4,1)} %bitcast.47), calls=%async_computation.4 | async-start | bytes 2523136
  550.2 9.7 %copy-start.7 = (bf16[3546,384]{0,1:T(8,128)(2,1)S(1)}, bf16[3546,384]{0,1:T(8,128)(2,1)}, u32[]{:S(2)}) copy-start(bf16[3546,384]{0,1:T(8,128)(2,1)} %copy-done.6) | copy-start | bytes 8169988
  561.6 7.5 copy-start.23
  569.0 5.1 copy-start.28
  595.3 4.6 copy-start.44
  610.5 2.3 copy-start.35
  610.5 2.3 copy-start.38
  610.5 2.3 copy-start.42
  610.5 2.3 copy-start.37
  610.5 2.3 copy-start.46
  610.6 2.3 copy-start.47
Sparse Core Ops, SparseCore 0:
  10.9 56.6 all-gather.4
  70.4 54.3 all-gather.6
  586.2 162.2 all-reduce.12
where the time goes:
time: 767 us; the launch traced here: 761 us
  matrix products  235 us (31%)
  local copies, waits for them, and re-layouts  178 us (23%)
  blocking collectives  164 us (21%)
  waiting for transfers between devices  97.9 us (13%)
  other arithmetic  70.9 us (9%)
  between operations  14.8 us (2%)
    unnamed x4, waiting for transfers between devices  97.9 us
    unnamed x2, blocking collectives  80.1 us
    dot_general x4, matrix products, matmul(): return jnp.dot(left, right, preferred_element_type=jnp.float32)  78.5 us
    dot_general x4, matrix products, across_cols(): lax.dot_general(left, right, (((1,), (1,)), ((), ())), preferred_element_...  49.9 us
    all_gather x1, blocking collectives, local(): lax.all_gather(qkv_weight, 'dev', axis=0, tiled=True)  45.9 us
    all_gather x1, blocking collectives, local(): lax.all_gather(out_weight, 'dev', axis=0, tiled=True)  38.5 us
    dot_general x4, matrix products, across_rows(): lax.dot_general(left, right, (((0,), (0,)), ((), ())), preferred_element_...  33.5 us
    unnamed x132, local copies, waits for them, and re-layouts  24 us
  transfers between devices with their start and end apart: 3, of which 1 were waited for; matrix products, arithmetic and copies ran while one was open for 32% of the time, Pallas kernels for 0%

commit v1 on v0

v1 whole, which is shorter than its diff:
```python
import functools
import jax
import jax.numpy as jnp
from jax import lax
from jax.experimental import pallas as pl
from jax.experimental.pallas import tpu as pltpu
from jax.sharding import PartitionSpec as P

D, HEADS, HEAD_DIM, FF = 384, 6, 64, 1536
EPS = 1e-6
F32, BF16 = jnp.float32, jnp.bfloat16
RS2 = 0.7071067811865476
RS2PI = 0.3989422804014327
VM = pltpu.VMEM


def nn(a, b):
    return lax.dot_general(a, b, (((1,), (0,)), ((), ())), preferred_element_type=F32)


def nt(a, b):
    return lax.dot_general(a, b, (((1,), (1,)), ((), ())), preferred_element_type=F32)


def tn(a, b):
    return lax.dot_general(a, b, (((0,), (0,)), ((), ())), preferred_element_type=F32)


def col8(v):
    return v.reshape(v.shape[0] // 8, 8, v.shape[1]).sum(axis=0)


def norm_fwd(v):
    c = v - jnp.mean(v, axis=1, keepdims=True)
    r = lax.rsqrt(jnp.mean(c * c, axis=1, keepdims=True) + EPS)
    return c * r, r


def norm_bwd(g, n, r, gain):
    e = g * gain
    return r * (e - jnp.mean(e, axis=1, keepdims=True) - n * jnp.mean(e * n, axis=1, keepdims=True))


def fused_kernel(L, LP, QP, CH, valid, x_ref, c_ref, wqkv, wo, w1, w2, nrm, bia, bhid,
                 out_ref, dx_ref, gqkv, gout, gfc1, gfc2, gsm,
                 xp, cp, n1s, r1s, h1s, qs, ks, vs, ps, os_, x1s, n2s, h2s, as_, gzs, gos, gts):
    i = pl.program_id(0)

    @pl.when(i == 0)
    def _():
        for r in (gqkv, gout, gfc1, gfc2, gsm):
            r[...] = jnp.zeros_like(r)
        xp[...] = jnp.zeros_like(xp)
        cp[...] = jnp.zeros_like(cp)
        qs[...] = jnp.zeros_like(qs)
        gos[...] = jnp.zeros_like(gos)

    mask = valid[i].astype(F32)
    g1, c1, g2, c2 = (nrm[j:j + 1, :] for j in range(4))
    bq, bv, bo, b2 = (bia[j:j + 1, :] for j in range(4))
    lane = lax.broadcasted_iota(jnp.int32, (1, 128), 1)
    low = lane < 64

    xp[:L, :] = x_ref[0]
    cp[:L, :] = c_ref[0]

    def stacked(ref, cols):
        v = ref[:, cols]
        z = jnp.zeros_like(v)
        return jnp.concatenate([jnp.where(low, v, z), jnp.where(low, z, v)], axis=0)

    n1, r1 = norm_fwd(xp[...].astype(F32))
    n1s[...] = n1
    r1s[...] = r1
    h1s[...] = (n1 * g1 + c1).astype(BF16)
    t = nn(h1s[...], wqkv[...])
    qs[:LP, :] = (t[:, :D] + bq).astype(BF16) * BF16(0.125)
    ks[...] = t[:, D:2 * D].astype(BF16)
    vs[...] = (t[:, 2 * D:] + bv).astype(BF16)
    for j in range(HEADS // 2):
        cols = slice(128 * j, 128 * j + 128)
        st = nt(ks[:, cols], stacked(qs, cols))
        top, bot = st[:LP - 16], st[LP - 16:]
        row = lax.broadcasted_iota(jnp.int32, bot.shape, 0) + (LP - 16)
        bot = jnp.where(row < L, bot, -1e30)
        mx = jnp.maximum(jnp.max(top, axis=0, keepdims=True), jnp.max(bot, axis=0, keepdims=True))
        e = jnp.exp(jnp.concatenate([top, bot], axis=0) - mx)
        p = e * (1.0 / jnp.sum(e, axis=0, keepdims=True))
        ps[j] = p.astype(BF16)
        o2 = tn(ps[j], vs[:, cols])
        os_[:, cols] = jnp.where(low, o2[:LP], o2[QP:QP + LP]).astype(BF16)
    x1 = xp[...].astype(F32) + nn(os_[...], wo[...]) + bo
    x1s[...] = x1
    n2, r2 = norm_fwd(x1)
    n2s[...] = n2
    h2s[...] = (n2 * g2 + c2).astype(BF16)

    gyb = cp[...] * mask.astype(BF16)
    for c in range(FF // CH):
        cols = slice(c * CH, (c + 1) * CH)
        z = nn(h2s[...], w1[:, cols]) + bhid[:, cols]
        ga = nt(gyb, w2[cols, :])
        phi = 0.5 + 0.5 * lax.erf(z * RS2)
        as_[:, cols] = (z * phi).astype(BF16)
        gz = ga * (phi + z * (RS2PI * jnp.exp(-0.5 * z * z)))
        gsm[:, 7 * D + c * CH:7 * D + (c + 1) * CH] += col8(gz)
        gzs[:, cols] = gz.astype(BF16)
    y = (x1s[...] + nn(as_[...], w2[...]) + b2) * mask
    out_ref[0] = y[:L].astype(BF16)
    gfc2[...] += tn(as_[...], gyb)
    gfc1[...] += tn(h2s[...], gzs[...])
    gh2 = nt(gzs[...], w1[...])
    n2 = n2s[...]
    gy = gyb.astype(F32)
    gsm[:, 2 * D:3 * D] += col8(gh2 * n2)
    gsm[:, 3 * D:4 * D] += col8(gh2)
    gsm[:, 7 * D + FF:] += col8(gy)
    gx1 = gy + norm_bwd(gh2, n2, r2, g2)
    x1s[...] = gx1
    gsm[:, 6 * D:7 * D] += col8(gx1)
    gx1b = gx1.astype(BF16)
    gout[...] += tn(os_[...], gx1b)
    gos[:LP, :] = nt(gx1b, wo[...]).astype(BF16)

    for j in range(HEADS // 2):
        cols = slice(128 * j, 128 * j + 128)
        p = ps[j]
        gv = jnp.where(low, nn(p[:, :QP], gos[:, cols]), nn(p[:, QP:], gos[:, cols]))
        gp = nt(vs[:, cols], stacked(gos, cols))
        pf = p.astype(F32)
        gs = (pf * (gp - jnp.sum(gp * pf, axis=0, keepdims=True))).astype(BF16)
        q2 = tn(gs, ks[:, cols])
        gq = jnp.where(low, q2[:LP], q2[QP:QP + LP]) * 0.125
        gk = jnp.where(low, nn(gs[:, :QP], qs[:, cols]), nn(gs[:, QP:], qs[:, cols]))
        gsm[:, 4 * D + 128 * j:4 * D + 128 * j + 128] += col8(gq)
        gsm[:, 5 * D + 128 * j:5 * D + 128 * j + 128] += col8(gv)
        gts[:, 128 * j:128 * j + 128] = gq.astype(BF16)
        gts[:, D + 128 * j:D + 128 * j + 128] = gk.astype(BF16)
        gts[:, 2 * D + 128 * j:2 * D + 128 * j + 128] = gv.astype(BF16)
    gqkv[...] += tn(h1s[...], gts[...])
    gh1 = nt(gts[...], wqkv[...])
    n1 = n1s[...]
    gsm[:, :D] += col8(gh1 * n1)
    gsm[:, D:2 * D] += col8(gh1)
    dx = x1s[...] + norm_bwd(gh1, n1, r1s[...], g1)
    dx_ref[0] = dx[:L]


def fused(tokens, cot, valid, wqkv, wo, w1, w2, nrm, bia, bhid):
    N, L, _ = tokens.shape
    LP = -(-L // 16) * 16
    QP = -(-L // 128) * 128
    const = lambda *s: pl.BlockSpec(s, lambda i, v: (0,) * len(s), pipeline_mode=pl.Buffered(1))
    img = lambda: pl.BlockSpec((1, L, D), lambda i, v: (i, 0, 0))
    grid_spec = pltpu.PrefetchScalarGridSpec(
        num_scalar_prefetch=1, grid=(N,),
        in_specs=[img(), img(), const(D, 3 * D), const(D, D), const(D, FF), const(FF, D),
                  const(4, D), const(4, D), const(1, FF)],
        out_specs=[img(), img(), const(D, 3 * D), const(D, D), const(D, FF), const(FF, D), const(8, 8 * D + FF)],
        scratch_shapes=[
            VM((LP, D), BF16), VM((LP, D), BF16), VM((LP, D), F32), VM((LP, 1), F32), VM((LP, D), BF16),
            VM((QP, D), BF16), VM((LP, D), BF16), VM((LP, D), BF16), VM((HEADS // 2, LP, 2 * QP), BF16),
            VM((LP, D), BF16), VM((LP, D), F32), VM((LP, D), F32), VM((LP, D), BF16),
            VM((LP, FF), BF16), VM((LP, FF), BF16), VM((QP, D), BF16), VM((LP, 3 * D), BF16)])
    sds = jax.ShapeDtypeStruct
    return pl.pallas_call(
        functools.partial(fused_kernel, L, LP, QP, 512),
        grid_spec=grid_spec,
        out_shape=[sds((N, L, D), BF16), sds((N, L, D), F32), sds((D, 3 * D), F32), sds((D, D), F32),
                   sds((D, FF), F32), sds((FF, D), F32), sds((8, 8 * D + FF), F32)],
        compiler_params=pltpu.CompilerParams(vmem_limit_bytes=60 << 20),
    )(valid, tokens, cot, wqkv, wo, w1, w2, nrm, bia, bhid)


def local(tokens, cotangent, valid_slots, qkv_weight, out_weight, fc1_weight, fc2_weight, norm_params, bias_params):
    ag = lambda v: lax.all_gather(v, "dev", axis=0, tiled=True)
    rs = lambda v: lax.psum_scatter(v, "dev", scatter_dimension=0, tiled=True)
    wqkv = ag(qkv_weight).reshape(D, 3 * D)
    wo = ag(out_weight).reshape(D, D)
    w1 = ag(fc1_weight).reshape(D, FF)
    w2 = ag(fc2_weight).reshape(FF, D)
    nrm = ag(norm_params).astype(F32).reshape(4, D)
    b = ag(bias_params).astype(F32)
    bia = jnp.concatenate([b[:3 * D], b[3 * D + FF:]]).reshape(4, D)
    bhid = b[3 * D:3 * D + FF].reshape(1, FF)
    out, dx, gqkv, gout, gfc1, gfc2, gsm = fused(tokens, cotangent, valid_slots, wqkv, wo, w1, w2, nrm, bia, bhid)
    gsm = jnp.sum(gsm, axis=0)
    return (out, dx, rs(gqkv.reshape(-1)), rs(gout.reshape(-1)), rs(gfc1.reshape(-1)), rs(gfc2.reshape(-1)),
            rs(gsm[:4 * D]), rs(gsm[4 * D:]))


def solution(mesh):
    s3, s1 = P("dev", None, None), P("dev")
    return jax.shard_map(local, mesh=mesh, in_specs=(s3, s3) + (s1,) * 7, out_specs=(s3, s3) + (s1,) * 6, check_vma=False)
```

time: 767 us -> 476 us (0.62)
  matrix products: 235 us -> 0 us
  local copies, waits for them, and re-layouts: 178 us -> 32.4 us
  Pallas kernels: 0 us -> 132 us
  other arithmetic: 70.9 us -> 7.1 us
  waiting for transfers between devices: 97.9 us -> 123 us
    dot_general x18 -> x0, matrix products: 235 us -> none  [the longest x4 78.5 us: matmul(): return jnp.dot(left, right, preferred_element_type=jnp.float32)]
    pallas_call x0 -> x1, Pallas kernels: none -> 132 us  [fused(): pl.pallas_call(functools.partial(fused_kernel, L, LP, QP, 512), grid_spec...]
    reshape x22 -> x11, local copies, waits for them, and re-layouts: 111 us -> 21.2 us  [the longest x1 3.47 us: local(): w1 = ag(fc1_weight).reshape(D, FF)]
    reduce_sum x8 -> x1, other arithmetic: 32.1 us -> 0.04 us  [local(): gsm = jnp.sum(gsm, axis=0)]
    unnamed x4, waiting for transfers between devices: 97.9 us -> 123 us
    convert_element_type x5 -> x0, local copies, waits for them, and re-layouts: 22.4 us -> none  [the longest x2 12.9 us: local(): mixed_low = mixed.reshape(rows_total, D).astype(jnp.bfloat16)]
    convert_element_type x4 -> x0, other arithmetic: 21 us -> none  [the longest x1 15.2 us: local(): grad_scores_low = grad_scores.astype(jnp.bfloat16)]
    unnamed x132 -> x16, local copies, waits for them, and re-layouts: 24 us -> 11.3 us
  transfers between devices with their start and end apart: 3 -> 3, of which waited for: 1 -> 1; matrix products, arithmetic and copies ran while one was open for 32% -> 4% of each run, Pallas kernels for 0% -> 0%
where the time goes in v1:
time: 476 us; the launch traced here: 475 us
  blocking collectives  166 us (35%)
  Pallas kernels  132 us (28%)
  waiting for transfers between devices  123 us (26%)
  local copies, waits for them, and re-layouts  32.4 us (7%)
  between operations  13.8 us (3%)
  other arithmetic  7.1 us (1%)
    pallas_call x1, Pallas kernels, fused(): pl.pallas_call(functools.partial(fused_kernel, L, LP, QP, 512), grid_spec...  132 us
    unnamed x4, waiting for transfers between devices  123 us
    all_gather x2, blocking collectives, local(): ag = lambda v: lax.all_gather(v, 'dev', axis=0, tiled=True)  84.5 us
    unnamed x2, blocking collectives  81.7 us
    unnamed x16, local copies, waits for them, and re-layouts  11.3 us
  transfers between devices with their start and end apart: 3, of which 1 were waited for; matrix products, arithmetic and copies ran while one was open for 4% of the time, Pallas kernels for 0%

profile of v1, /device:TPU:0, one launch (start us, length us, event | category | flops | bytes accessed | tf_op | source)
XLA Modules:
  0.0 474.9 jit_solution(1579539782312786129)
XLA Ops:
  7.2 0.0 all-gather.5.cloned.1.call-start
  7.2 0.7 all-gather.5.cloned.1.call-update
  7.9 0.0 all-gather.7.cloned.1.call-start
  7.9 0.7 all-gather.7.cloned.1.call-update
  8.6 0.0 all-reduce.13.cloned.1.call-start
  8.7 0.9 dynamic-update-slice
  9.6 0.8 dynamic-update-slice.1
  10.4 42.2 %all-reduce.10 = (bf16[1536]{0:T(1024)(128)(2,1)S(1)}, bf16[3072]{0:T(1024)(128)(2,1)S(1)}) all-reduce(bf16[1536]{0:T(1024)(128)(2,1)S(1)} %dynamic-update-slice, bf16[3072]{0:T(1024)(128)(2,1)S(1)} %dynamic-update-slice.1), channel_id=1, replica_groups=mesh['dev'=32] {'dev'}, use_global_device_ids=true, to_apply=%add | all-reduce | flops 4608 | bytes 18432
  52.6 0.6 reshape.64.nrm
  53.2 0.6 reshape.57.bia
  53.8 0.6 reshape.58.bhid
  54.4 0.7 reshape.71
  55.2 0.8 reshape.69
  55.9 42.0 %all-gather.1 = bf16[32,1,4608]{2,1,0:T(2,128)(2,1)S(1)} all-gather(bf16[1,1,4608]{2,1,0:T(2,128)(2,1)S(1)} %reshape.71), channel_id=1, replica_groups=mesh['dev'=32] {'dev'}, dimensions={0}, use_global_device_ids=true | all-gather | bytes 304128 | tf_op jit(solution)/shard_map/all_gather | solution.py:176
  97.9 1.7 reduce.1
  99.7 1.1 reshape.52.wo
  100.7 42.5 %all-gather = bf16[32,1,13824]{2,1,0:T(2,128)(2,1)S(1)} all-gather(bf16[1,1,13824]{2,1,0:T(2,128)(2,1)S(1)} %reshape.69), channel_id=1, replica_groups=mesh['dev'=32] {'dev'}, dimensions={0}, use_global_device_ids=true | all-gather | bytes 912384 | tf_op jit(solution)/shard_map/all_gather | solution.py:176
  143.3 5.3 %reduce = bf16[32,13824]{1,0:T(8,128)(2,1)S(1)} reduce(bf16[32,1,13824]{2,1,0:T(2,128)(2,1)S(1)} %all-gather, bf16[]{:T(256)} %constant.32), dimensions={1}, to_apply=%all-gather.reduce_sub_computation | reduce | bytes 1769474 | tf_op jit(solution)/shard_map/all_gather | solution.py:176
  148.6 2.4 reshape.51.wqkv
  150.9 0.0 all-gather.5.cloned.1.call-done
  150.9 3.5 reshape.53.w1
  154.4 0.0 all-gather.7.cloned.1.call-done
  154.4 3.1 reshape.54.w2
  157.5 131.7 %shard_map.152 = (bf16[18,197,384]{2,1,0:T(8,128)(2,1)}, f32[18,197,384]{2,1,0:T(8,128)}, f32[384,1152]{1,0:T(8,128)}, f32[384,384]{1,0:T(8,128)}, f32[384,1536]...) custom-call(s32[18]{0:T(128)} %valid.1, bf16[18,197,384]{2,1,0:T(8,128)(2,1)} %x_ref.1, ...), custom_call_target="tpu_custom_call" | custom-call | tf_op jit(solution)/shard_map/pallas_call | solution.py:166
  289.1 2.0 reshape.60
  291.1 2.5 reshape.59
  293.6 0.0 copy-start
  293.6 3.3 reshape.61
  297.0 0.0 copy-done
  297.0 1.6 reshape.62
  298.6 0.0 copy-start.1
  298.6 0.0 all-reduce.13.cloned.1.call-update
  298.6 0.9 copy-done.1
  299.5 39.5 %all-reduce.8 = (f32[1536]{0:T(1024)S(1)}, f32[3072]{0:T(1024)S(1)}) all-reduce(f32[1536]{0:T(1024)S(1)} %slice.23, f32[3072]{0:T(1024)S(1)} %slice.24), channel_id=6, replica_groups=mesh['dev'=32] {'dev'}, use_global_device_ids=true, to_apply=%region_5.0.clone | all-reduce | flops 4608 | bytes 36864
  339.1 0.6 dynamic-slice.4
  339.7 0.6 dynamic-slice.5
  340.3 122.1 %all-reduce.13.cloned.1.call-done = (f32[442368]{0:T(1024)}, f32[147456]{0:T(1024)}, f32[589824]{0:T(1024)}, f32[589824]{0:T(1024)}) async-done(((f32[442368]{0:T(1024)}, f32[147456]{0:T(1024)}, f32[589824]{0:T(1024)}, f32[589824]{0:T(1024)}), (f32[442368]{0:T(1024)}, f32[147456]{0:T(1024)}, f32[589824]{0:T(1024)}, f32[589824]{0:T(1024)})) %all-reduce.13.cloned.1.call-update) | async-done | bytes 7077904
  462.3 1.5 dynamic-slice.2
  463.8 1.5 dynamic-slice.3
  465.4 1.5 dynamic-slice
  466.9 1.4 dynamic-slice.1
  (9 shorter events, 0.1 us)
Async XLA Ops:
  7.2 143.8 %all-gather.5.cloned.1.call-start = ((), (), s32[]{:S(2)}) async-start(), calls=%async_computation | async-start | bytes 1216512 | tf_op jit(solution)/shard_map/all_gather | solution.py:176
  7.9 146.5 %all-gather.7.cloned.1.call-start = ((), (), s32[]{:S(2)}) async-start(), calls=%async_computation.1 | async-start | bytes 1216512 | tf_op jit(solution)/shard_map/all_gather | solution.py:176
  8.6 453.7 %all-reduce.13.cloned.1.call-start = ((), (), s32[]{:S(2)}) async-start(), calls=%async_computation.2 | async-start | bytes 14155776
  293.6 3.3 copy-start
  298.6 0.9 copy-start.1
Sparse Core Ops, SparseCore 0:
  10.9 56.6 all-gather.4
  70.5 54.6 all-gather.6
  298.7 163.5 all-reduce.12

commit v2 on v1

v2 whole, which is shorter than its diff:
```python
import functools
import jax
import jax.numpy as jnp
from jax import lax
from jax.experimental import pallas as pl
from jax.experimental.pallas import tpu as pltpu
from jax.sharding import PartitionSpec as P

D, HEADS, HEAD_DIM, FF = 384, 6, 64, 1536
PAIRS = HEADS // 2
EPS = 1e-6
F32, BF16 = jnp.float32, jnp.bfloat16
RS2 = 0.7071067811865476
RS2PI = 0.3989422804014327
VM = pltpu.VMEM
BIAS_ROW = 16
SDS = jax.ShapeDtypeStruct


def nn(a, b):
    return lax.dot_general(a, b, (((1,), (0,)), ((), ())), preferred_element_type=F32)


def nt(a, b):
    return lax.dot_general(a, b, (((1,), (1,)), ((), ())), preferred_element_type=F32)


def tn(a, b):
    return lax.dot_general(a, b, (((0,), (0,)), ((), ())), preferred_element_type=F32)


def col8(v):
    return v.reshape(v.shape[0] // 8, 8, v.shape[1]).sum(axis=0)


def norm_fwd(v):
    c = v - jnp.mean(v, axis=1, keepdims=True)
    r = lax.rsqrt(jnp.mean(c * c, axis=1, keepdims=True) + EPS)
    return c * r, r


def norm_bwd(g, n, r, gain):
    e = g * gain
    return r * (e - jnp.mean(e, axis=1, keepdims=True) - n * jnp.mean(e * n, axis=1, keepdims=True))


def vec(sml, row, count=3):
    return jnp.concatenate([sml[row + j:row + j + 1, :] for j in range(count)], axis=1)


def low_lanes():
    return lax.broadcasted_iota(jnp.int32, (1, 128), 1) < 64


def stacked(v):
    low, z = low_lanes(), jnp.zeros_like(v)
    return jnp.concatenate([jnp.where(low, v, z), jnp.where(low, z, v)], axis=0)


class Pad:
    def __init__(self, tokens):
        self.n, self.len, _ = tokens.shape
        self.rows = -(-self.len // 16) * 16
        self.lanes = -(-self.len // 128) * 128

    def step(self, most):
        return max(b for b in range(1, most + 1) if self.n % b == 0)


def attn_fwd(s, b, x_ref, wqkv, sml, q_ref, k_ref, v_ref, p_ref, o_ref, xp, h1, ks, vs):
    lp, qp, low = s.rows, s.lanes, low_lanes()
    for u in range(b):
        xp[u * lp:u * lp + s.len, :] = x_ref[u]
    n1, _ = norm_fwd(xp[...].astype(F32))
    h1[...] = (n1 * vec(sml, 0) + vec(sml, 3)).astype(BF16)
    t = nn(h1[...], wqkv[...])
    q = (t[:, :D] + vec(sml, BIAS_ROW)).astype(BF16) * BF16(0.125)
    k = t[:, D:2 * D].astype(BF16)
    v = (t[:, 2 * D:] + vec(sml, BIAS_ROW + 3)).astype(BF16)
    for u in range(b):
        rows = slice(u * lp, u * lp + lp)
        q_ref[u, :lp, :] = q[rows]
        q_ref[u, lp:, :] = jnp.zeros((qp - lp, D), BF16)
        k_ref[u] = k[rows]
        v_ref[u] = v[rows]
    for u in range(b):
        for j in range(PAIRS):
            cols = slice(128 * j, 128 * j + 128)
            st = nt(k_ref[u, :, cols], stacked(q_ref[u, :, cols]))
            top, bot = st[:lp - 16], st[lp - 16:]
            row = lax.broadcasted_iota(jnp.int32, bot.shape, 0) + (lp - 16)
            bot = jnp.where(row < s.len, bot, -1e30)
            mx = jnp.maximum(jnp.max(top, axis=0, keepdims=True), jnp.max(bot, axis=0, keepdims=True))
            e = jnp.exp(jnp.concatenate([top, bot], axis=0) - mx)
            p = e * (1.0 / jnp.sum(e, axis=0, keepdims=True))
            p_ref[u, j] = p.astype(BF16)
            o2 = tn(p_ref[u, j], v_ref[u, :, cols])
            o_ref[u, :, cols] = jnp.where(low, o2[:lp], o2[qp:qp + lp]).astype(BF16)


def ffn(s, b, ch, i, valid, x_ref, c_ref, o_ref, wo, w1, w2, sml,
        out_ref, gx_ref, go_ref, gout, gfc1, gfc2, gsm, xp, cp, os_, n2s, h2s, as_, gzs, x1s):
    lp, qp = s.rows, s.lanes
    g2, c2 = vec(sml, 6), vec(sml, 9)
    bo, bh, b2 = vec(sml, BIAS_ROW + 6), vec(sml, BIAS_ROW + 9, 12), vec(sml, BIAS_ROW + 21)
    for u in range(b):
        xp[u * lp:u * lp + s.len, :] = x_ref[u]
        cp[u * lp:u * lp + s.len, :] = c_ref[u] * valid[i * b + u].astype(BF16)
        os_[u * lp:u * lp + lp, :] = o_ref[u]
    x1 = xp[...].astype(F32) + nn(os_[...], wo[...]) + bo
    x1s[...] = x1
    n2, r2 = norm_fwd(x1)
    n2s[...] = n2
    h2s[...] = (n2 * g2 + c2).astype(BF16)
    for c in range(FF // ch):
        cols = slice(c * ch, (c + 1) * ch)
        z = nn(h2s[...], w1[:, cols]) + bh[:, cols]
        ga = nt(cp[...], w2[cols, :])
        phi = 0.5 + 0.5 * lax.erf(z * RS2)
        as_[:, cols] = (z * phi).astype(BF16)
        gz = ga * (phi + z * (RS2PI * jnp.exp(-0.5 * z * z)))
        gsm[:, 7 * D + c * ch:7 * D + (c + 1) * ch] += col8(gz)
        gzs[:, cols] = gz.astype(BF16)
    y = x1s[...] + nn(as_[...], w2[...]) + b2
    for u in range(b):
        out_ref[u] = (y[u * lp:u * lp + s.len] * valid[i * b + u].astype(F32)).astype(BF16)
    gfc2[...] += tn(as_[...], cp[...])
    gfc1[...] += tn(h2s[...], gzs[...])
    gh2 = nt(gzs[...], w1[...])
    n2 = n2s[...]
    gy = cp[...].astype(F32)
    gsm[:, 2 * D:3 * D] += col8(gh2 * n2)
    gsm[:, 3 * D:4 * D] += col8(gh2)
    gsm[:, 7 * D + FF:] += col8(gy)
    gx1 = gy + norm_bwd(gh2, n2, r2, g2)
    gsm[:, 6 * D:7 * D] += col8(gx1)
    gx1b = gx1.astype(BF16)
    gout[...] += tn(os_[...], gx1b)
    go = nt(gx1b, wo[...]).astype(BF16)
    for u in range(b):
        gx_ref[u] = gx1[u * lp:u * lp + lp]
        go_ref[u, :lp, :] = go[u * lp:u * lp + lp]
        go_ref[u, lp:, :] = jnp.zeros((qp - lp, D), BF16)


def attn_bwd(s, b, q_ref, k_ref, v_ref, p_ref, go_ref, gt_ref, gqv):
    lp, qp, low = s.rows, s.lanes, low_lanes()
    for u in range(b):
        for j in range(PAIRS):
            cols = slice(128 * j, 128 * j + 128)
            p, go = p_ref[u, j], go_ref[u, :, cols]
            gv = jnp.where(low, nn(p[:, :qp], go), nn(p[:, qp:], go))
            gp = nt(v_ref[u, :, cols], stacked(go))
            pf = p.astype(F32)
            gs = (pf * (gp - jnp.sum(gp * pf, axis=0, keepdims=True))).astype(BF16)
            q2 = tn(gs, k_ref[u, :, cols])
            gq = jnp.where(low, q2[:lp], q2[qp:qp + lp]) * 0.125
            q = q_ref[u, :, cols]
            gk = jnp.where(low, nn(gs[:, :qp], q), nn(gs[:, qp:], q))
            gqv[:, 128 * j:128 * j + 128] += col8(gq)
            gqv[:, D + 128 * j:D + 128 * j + 128] += col8(gv)
            gt_ref[u, :, 128 * j:128 * j + 128] = gq.astype(BF16)
            gt_ref[u, :, D + 128 * j:D + 128 * j + 128] = gk.astype(BF16)
            gt_ref[u, :, 2 * D + 128 * j:2 * D + 128 * j + 128] = gv.astype(BF16)


def proj_bwd(s, b, x_ref, gt_ref, gx_ref, wqkv, sml, dx_ref, gqkv, gn1, xp, h1, gts):
    lp = s.rows
    g1 = vec(sml, 0)
    for u in range(b):
        xp[u * lp:u * lp + s.len, :] = x_ref[u]
        gts[u * lp:u * lp + lp, :] = gt_ref[u]
    n1, r1 = norm_fwd(xp[...].astype(F32))
    h1[...] = (n1 * g1 + vec(sml, 3)).astype(BF16)
    gqkv[...] += tn(h1[...], gts[...])
    gh1 = nt(gts[...], wqkv[...])
    gn1[:, :D] += col8(gh1 * n1)
    gn1[:, D:] += col8(gh1)
    back = norm_bwd(gh1, n1, r1, g1)
    for u in range(b):
        dx_ref[u] = gx_ref[u, :s.len] + back[u * lp:u * lp + s.len]


def zero(*refs):
    for r in refs:
        r[...] = jnp.zeros_like(r)


def img(b, *shape):
    return pl.BlockSpec((b,) + shape, lambda i, *_: (i,) + (0,) * len(shape))


def const(*shape):
    return pl.BlockSpec(shape, lambda i, *_: (0,) * len(shape), pipeline_mode=pl.Buffered(1))


def big(**kw):
    return pltpu.CompilerParams(vmem_limit_bytes=62 << 20, **kw)


MESHID = pl.DeviceIdType.MESH


def chip_dims(n):
    chips = n // 2
    side = 4 if chips >= 64 else 2
    return (chips // (side * side), side, side)


class Place:
    def __init__(self, n):
        self.n, self.dims = n, chip_dims(n)
        me = lax.axis_index("dev")
        self.me, self.core = me, lax.rem(me, 2)
        s0, s1, s2 = self.dims
        chip = me // 2
        self.at = (chip // (s1 * s2), lax.rem(chip // s2, s1), lax.rem(chip, s2))
        self.offs = [(a, b, c) for a in range(s0) for b in range(s1) for c in range(s2)]

    def chip(self, off):
        i0, i1, i2 = (lax.rem(i + s + o, s) for i, s, o in zip(self.at, self.dims, off))
        return (i0 * self.dims[1] + i1) * self.dims[2] + i2

    def dev(self, off):
        return 2 * self.chip(off) + self.core

    def partner(self, off=(0, 0, 0)):
        return 2 * self.chip(off) + 1 - self.core

    def num(self, off):
        return (off[0] * self.dims[1] + off[1]) * self.dims[2] + off[2]

    def peers(self):
        for k in range(3):
            for o in range(1, self.dims[k]):
                yield self.dev(unit(k, o))
        yield self.partner()


def unit(k, o):
    return tuple(o if j == k else 0 for j in range(3))


def neg(off):
    return tuple(-o for o in off)


def greet(pl_):
    barrier = pltpu.get_barrier_semaphore()
    count = 0
    for dev in pl_.peers():
        pl.semaphore_signal(barrier, inc=1, device_id=(dev,), device_id_type=MESHID)
        count += 1
    pl.semaphore_wait(barrier, count)


ORDERS = ((0, 2, 1), (0, 1, 2))


class Gather:
    def __init__(self, place, src, buf, ssem, rsem):
        self.p, self.src, self.buf, self.ssem, self.rsem = place, src, buf, ssem, rsem
        self.half = src.shape[0] // 2

    def link(self, h, off, to, dev):
        p, rows = self.p, pl.ds(h * self.half, self.half)
        origin = p.dev(neg(off))
        src = self.src.at[rows] if not any(off) else self.buf.at[origin, rows]
        k = p.num(to)
        return pltpu.make_async_remote_copy(
            src_ref=src, dst_ref=self.buf.at[origin, rows], send_sem=self.ssem.at[0, h, k],
            recv_sem=self.rsem.at[0, h, k], device_id=(dev,), device_id_type=MESHID)

    def cross(self, h, off):
        p, rows = self.p, pl.ds(h * self.half, self.half)
        origin = p.dev(neg(off))
        src = self.src.at[rows] if not any(off) else self.buf.at[origin, rows]
        k = p.num(off)
        return pltpu.make_async_remote_copy(
            src_ref=src, dst_ref=self.buf.at[origin, rows], send_sem=self.ssem.at[1, h, k],
            recv_sem=self.rsem.at[1, h, k], device_id=(p.partner(),), device_id_type=MESHID)

    def hops(self, h, off):
        order = ORDERS[h]
        last = max([j for j in range(3) if off[order[j]]], default=-1)
        for j in range(last + 1, 3):
            k = order[j]
            for o in range(1, self.p.dims[k]):
                to = tuple(a + b for a, b in zip(off, unit(k, o)))
                yield to, self.p.dev(unit(k, o))

    def forward(self, h, off):
        for to, dev in self.hops(h, off):
            self.link(h, off, to, dev).start()
        self.cross(h, off).start()

    def begin(self):
        for h in range(2):
            self.forward(h, (0, 0, 0))

    def arrivals(self):
        offs = sorted([o for o in self.p.offs if any(o)], key=lambda o: (sum(1 for a in o if a), min(o[0], self.p.dims[0] - o[0])))
        return [(h, o) for o in offs for h in range(2)]

    def arrive(self, h, off):
        self.link(h, off, off, self.p.me).wait_recv()
        self.forward(h, off)

    def finish(self):
        for h in range(2):
            for off in self.p.offs:
                c = self.cross(h, off)
                c.wait_recv()
                c.wait_send()
                for to, dev in self.hops(h, off):
                    self.link(h, off, to, dev).wait_send()


class Reduce:
    def __init__(self, place, part, rc, rb, ssem, rsem):
        self.p, self.part, self.rc, self.rb, self.ssem, self.rsem = place, part, rc, rb, ssem, rsem
        self.half = part.shape[1] // 2

    def rows(self, h):
        return pl.ds(h * self.half, self.half)

    def cross(self, h, off):
        p, k = self.p, self.p.num(off)
        return pltpu.make_async_remote_copy(
            src_ref=self.part.at[p.partner(off), self.rows(h)], dst_ref=self.rc.at[k, self.rows(h)],
            send_sem=self.ssem.at[1, h, k], recv_sem=self.rsem.at[1, h, k],
            device_id=(p.partner(),), device_id_type=MESHID)

    def step_dim(self, h, off):
        return [k for k in reversed(ORDERS[h]) if off[k]][0]

    def link(self, h, off):
        p, k = self.p, self.p.num(off)
        dim = self.step_dim(h, off)
        return pltpu.make_async_remote_copy(
            src_ref=self.part.at[p.dev(off), self.rows(h)], dst_ref=self.rb.at[k, self.rows(h)],
            send_sem=self.ssem.at[0, h, k], recv_sem=self.rsem.at[0, h, k],
            device_id=(p.dev(unit(dim, off[dim])),), device_id_type=MESHID)

    def sources(self, h, off):
        order = ORDERS[h]
        last = max([j for j in range(3) if off[order[j]]], default=-1)
        for j in reversed(range(last + 1, 3)):
            k = order[j]
            for o in range(1, self.p.dims[k]):
                yield tuple(a + b for a, b in zip(off, unit(k, o)))

    def order(self):
        offs = sorted(self.p.offs, key=lambda o: (-sum(1 for a in o if a), o))
        return [(h, o) for o in offs for h in range(2)]

    def begin(self):
        for h, off in self.order():
            self.cross(h, off).start()

    def total(self, h, off):
        p, k = self.p, self.p.num(off)
        self.cross(h, off).wait_recv()
        acc = self.part[p.dev(off), self.rows(h), :].astype(F32) + self.rc[k, self.rows(h), :].astype(F32)
        for s in self.sources(h, off):
            self.link(h, s).wait_recv()
            acc += self.rb[p.num(s), self.rows(h), :].astype(F32)
        return acc

    def advance(self, h, off):
        acc = self.total(h, off)
        if any(off):
            self.part[self.p.dev(off), self.rows(h), :] = acc.astype(BF16)
            self.link(h, off).start()
        return acc

    def finish(self):
        for h, off in self.order():
            self.cross(h, off).wait_send()
            if any(off):
                self.link(h, off).wait_send()


class Sizes:
    def __init__(self, n):
        up = lambda v, m: -(-v // m) * m
        self.n = n
        self.q, self.o, self.f = 3 * D * D // n // 128, D * D // n // 128, D * FF // n // 128
        self.norm, self.bias = 4 * D // n, (4 * D + FF) // n
        self.small = up(self.q, 16)
        self.r0 = up(self.small + 16, 32)
        self.f1 = up(self.o, 16)
        self.f2 = self.f1 + up(self.f, 16)
        self.r1 = up(self.f2 + up(self.f, 16), 32)


def sems(n):
    return [pltpu.SemaphoreType.DMA((2, 2, n // 2))] * 2


def levels(events):
    groups = {}
    for h, off in events:
        groups.setdefault(sum(1 for a in off if a), []).append((h, off))
    return groups


def at_step(i, k):
    return pl.when(i == k)


def unpack(z, buf, first, count, fl, w):
    def one(d, _):
        fl[pl.ds(d * count, count), :] = buf[d, first:first + -(-count // 16) * 16, :].astype(F32)[:count]
        return 0

    lax.fori_loop(0, z.n, one, 0)
    rows, cols = w.shape[0], w.shape[1] // 128
    for j in range(cols):
        w[:, 128 * j:128 * j + 128] = fl[pl.ds(j, rows, stride=cols), :].astype(BF16)


def unpack_small(z, buf, st, sml):
    lane = lax.broadcasted_iota(jnp.int32, (1, 128), 1)

    def put(v, d, size, base):
        shift, first = lax.rem(d * size, 128), d * size // 128
        v = pltpu.roll(v, shift, axis=1)
        sml[pl.ds(base + first, 1), :] += jnp.where(lane >= shift, v, 0.0)
        sml[pl.ds(base + first + 1, 1), :] += jnp.where(lane < shift, v, 0.0)

    def one(d, _):
        st[:16, :] = buf[d, z.small:z.small + 16, :].astype(F32)
        put(st[0:1, :], d, z.norm, 0)
        put(st[1:2, :], d, z.bias, BIAS_ROW)
        return 0

    lax.fori_loop(0, z.n, one, 0)


def flatten(g, fl):
    rows, cols = g.shape[0], g.shape[1] // 128
    for j in range(cols):
        fl[pl.ds(j, rows, stride=cols), :] = g[:, 128 * j:128 * j + 128]


def pack(z, fl, count, first, part):
    size = -(-count // 16) * 16

    def one(d, _):
        part[d, first:first + size, :] = fl[pl.ds(d * count, size), :].astype(BF16)
        return 0

    lax.fori_loop(0, z.n, one, 0)


def pack_small(z, gsm, gqv, gn1, sm, st, part):
    sm[...] = jnp.zeros_like(sm)
    st[...] = jnp.zeros_like(st)

    def put(ref, first, count, base):
        total = jnp.sum(ref[:, first:first + 128 * count], axis=0, keepdims=True)
        for j in range(count):
            sm[base + j:base + j + 1, :] = total[:, 128 * j:128 * j + 128]

    put(gn1, 0, 6, 0)
    put(gsm, 2 * D, 6, 6)
    put(gqv, 0, 6, BIAS_ROW)
    put(gsm, 6 * D, 18, BIAS_ROW + 6)
    lane = lax.broadcasted_iota(jnp.int32, (1, 128), 1)

    def take(d, size, base):
        shift, first = lax.rem(d * size, 128), d * size // 128
        v = jnp.where(lane >= shift, sm[pl.ds(base + first, 1), :], sm[pl.ds(base + first + 1, 1), :])
        return pltpu.roll(v, lax.rem(128 - shift, 128), axis=1)

    def one(d, _):
        st[0:1, :] = take(d, z.norm, 0)
        st[1:2, :] = take(d, z.bias, BIAS_ROW)
        part[d, z.small:z.small + 16, :] = st[:16, :].astype(BF16)
        return 0

    lax.fori_loop(0, z.n, one, 0)


def kernel1(n, s, b, x_ref, q_in, o_in, f1_in, f2_in, n_in, b_in, q_ref, k_ref, v_ref, p_ref, o_ref,
            wqkv, wo, w1, w2, sml, xp, h1, x0, x1, buf0, buf1, fl, st, s0, r0, s1, r1):
    i, last = pl.program_id(0), s.n // b - 1
    z = Sizes(n)
    place = Place(n)
    a, c = Gather(place, x0, buf0, s0, r0), Gather(place, x1, buf1, s1, r1)

    @pl.when(i == 0)
    def _():
        zero(xp, sml, st, x0, x1)
        st[0:1, :z.norm] = n_in[...].astype(F32)
        st[1:2, :z.bias] = b_in[...].astype(F32)
        x0[:z.q, :] = q_in[...]
        x0[z.small:z.small + 16, :] = st[:16, :].astype(BF16)
        x1[:z.o, :] = o_in[...]
        x1[z.f1:z.f1 + z.f, :] = f1_in[...]
        x1[z.f2:z.f2 + z.f, :] = f2_in[...]
        buf0[place.me] = x0[...]
        buf1[place.me] = x1[...]
        greet(place)
        a.begin()
        c.begin()
        for h, off in a.arrivals():
            a.arrive(h, off)
        a.finish()
        unpack_small(z, buf0, st, sml)
        unpack(z, buf0, 0, z.q, fl, wqkv)

    attn_fwd(s, b, x_ref, wqkv, sml, q_ref, k_ref, v_ref, p_ref, o_ref, xp, h1, None, None)

    for level, events in levels(c.arrivals()).items():
        @pl.when(i == min(2 * level, last))
        def _():
            for h, off in events:
                c.arrive(h, off)

    @pl.when(i == last)
    def _():
        c.finish()
        unpack(z, buf1, 0, z.o, fl, wo)
        unpack(z, buf1, z.f1, z.f, fl, w1)
        unpack(z, buf1, z.f2, z.f, fl, w2)


def call1(n, tokens, shards):
    s, z = Pad(tokens), Sizes(n)
    b = s.step(2)
    rows = b * s.rows
    saved = [((s.lanes, D), BF16), ((s.rows, D), BF16), ((s.rows, D), BF16), ((PAIRS, s.rows, 2 * s.lanes), BF16), ((s.rows, D), BF16)]
    whole = [((D, 3 * D), BF16), ((D, D), BF16), ((D, FF), BF16), ((FF, D), BF16), ((48, 128), F32)]
    return pl.pallas_call(
        functools.partial(kernel1, n, s, b), grid=(s.n // b,),
        in_specs=[img(b, s.len, D)] + [const(*v.shape) for v in shards],
        out_specs=[img(b, *v[0]) for v in saved] + [const(*v[0]) for v in whole],
        out_shape=[SDS((s.n,) + v[0], v[1]) for v in saved] + [SDS(*v) for v in whole],
        scratch_shapes=[VM((rows, D), BF16), VM((rows, D), BF16), VM((z.r0, 128), BF16), VM((z.r1, 128), BF16),
                        VM((n, z.r0, 128), BF16), VM((n, z.r1, 128), BF16), VM((4608 + 16, 128), F32), VM((16, 128), F32)] + sems(n) + sems(n),
        compiler_params=big(collective_id=0, has_side_effects=True))(tokens, *shards)


def kernel2(n, s, b, ch, valid, x_ref, c_ref, o_ref, wo, w1, w2, sml, out_ref, gx_ref, go_ref, part, gsm,
            xp, cp, os_, n2s, h2s, as_, gzs, x1s, gout, gfc1, gfc2, fl):
    i = pl.program_id(0)
    z = Sizes(n)

    @pl.when(i == 0)
    def _():
        zero(xp, cp, gout, gfc1, gfc2, gsm)

    ffn(s, b, ch, i, valid, x_ref, c_ref, o_ref, wo, w1, w2, sml,
        out_ref, gx_ref, go_ref, gout, gfc1, gfc2, gsm, xp, cp, os_, n2s, h2s, as_, gzs, x1s)

    @pl.when(i == s.n // b - 1)
    def _():
        zero(part)
        for g, count, first in ((gout, z.o, 0), (gfc1, z.f, z.f1), (gfc2, z.f, z.f2)):
            flatten(g, fl)
            pack(z, fl, count, first, part)


def call2(n, valid, tokens, cot, o, wo, w1, w2, sml):
    s, z = Pad(tokens), Sizes(n)
    b = s.step(3)
    rows = b * s.rows
    grid_spec = pltpu.PrefetchScalarGridSpec(
        num_scalar_prefetch=1, grid=(s.n // b,),
        in_specs=[img(b, s.len, D), img(b, s.len, D), img(b, s.rows, D), const(D, D), const(D, FF), const(FF, D), const(48, 128)],
        out_specs=[img(b, s.len, D), img(b, s.rows, D), img(b, s.lanes, D), const(n, z.r1, 128), const(8, 8 * D + FF)],
        scratch_shapes=[VM((rows, D), BF16), VM((rows, D), BF16), VM((rows, D), BF16), VM((rows, D), F32), VM((rows, D), BF16),
                        VM((rows, FF), BF16), VM((rows, FF), BF16), VM((rows, D), F32),
                        VM((D, D), F32), VM((D, FF), F32), VM((FF, D), F32), VM((4608 + 16, 128), F32)])
    return pl.pallas_call(
        functools.partial(kernel2, n, s, b, 256), grid_spec=grid_spec,
        out_shape=[SDS(tokens.shape, BF16), SDS((s.n, s.rows, D), F32), SDS((s.n, s.lanes, D), BF16),
                   SDS((n, z.r1, 128), BF16), SDS((8, 8 * D + FF), F32)],
        compiler_params=big())(valid, tokens, cot, o, wo, w1, w2, sml)


def kernel3(n, s, b, q_ref, k_ref, v_ref, p_ref, go_ref, part_in, gt_ref, gqv, res, part, rc, rb, s1, r1, local):
    i, last = pl.program_id(0), s.n // b - 1
    place = Place(n)
    r = Reduce(place, part, rc, rb, s1, r1)

    @pl.when(i == 0)
    def _():
        copy = pltpu.make_async_copy(part_in, part, local)
        copy.start()
        zero(gqv)
        greet(place)
        copy.wait()
        r.begin()

    attn_bwd(s, b, q_ref, k_ref, v_ref, p_ref, go_ref, gt_ref, gqv)

    for level, events in levels(r.order()).items():
        @pl.when(i == min(1 + 2 * (3 - level), last))
        def _():
            for h, off in events:
                acc = r.advance(h, off)
                if not any(off):
                    res[r.rows(h), :] = acc

    @pl.when(i == last)
    def _():
        r.finish()


def call3(n, s, q, k, v, p, go, part):
    z = Sizes(n)
    b = s.step(2)
    c = n // 2
    return pl.pallas_call(
        functools.partial(kernel3, n, s, b), grid=(s.n // b,),
        in_specs=[img(b, s.lanes, D), img(b, s.rows, D), img(b, s.rows, D), img(b, PAIRS, s.rows, 2 * s.lanes), img(b, s.lanes, D),
                  pl.BlockSpec(memory_space=pl.ANY)],
        out_specs=[img(b, s.rows, 3 * D), const(8, 2 * D), const(z.r1, 128)],
        out_shape=[SDS((s.n, s.rows, 3 * D), BF16), SDS((8, 2 * D), F32), SDS((z.r1, 128), F32)],
        scratch_shapes=[VM((n, z.r1, 128), BF16), VM((c, z.r1, 128), BF16), VM((c, z.r1, 128), BF16)] + sems(n) + [pltpu.SemaphoreType.DMA],
        compiler_params=big(collective_id=1, has_side_effects=True))(q, k, v, p, go, part)


def kernel4(n, s, b, x_ref, gt_ref, gx_ref, wqkv, sml, gsm, gqv, res, dx_ref, part, oo, o1, o2, gqkv, gn1, xp, h1, gts, fl, sm, st):
    i = pl.program_id(0)
    z = Sizes(n)

    @pl.when(i == 0)
    def _():
        zero(xp, gqkv, gn1)
        oo[...] = res[:z.o, :]
        o1[...] = res[z.f1:z.f1 + z.f, :]
        o2[...] = res[z.f2:z.f2 + z.f, :]

    proj_bwd(s, b, x_ref, gt_ref, gx_ref, wqkv, sml, dx_ref, gqkv, gn1, xp, h1, gts)

    @pl.when(i == s.n // b - 1)
    def _():
        zero(part)
        flatten(gqkv, fl)
        pack(z, fl, z.q, 0, part)
        pack_small(z, gsm, gqv, gn1, sm, st, part)


def call4(n, tokens, gt, gx, wqkv, sml, gsm, gqv, res):
    s, z = Pad(tokens), Sizes(n)
    b = s.step(3)
    rows = b * s.rows
    shards = [(z.o, 128), (z.f, 128), (z.f, 128)]
    return pl.pallas_call(
        functools.partial(kernel4, n, s, b), grid=(s.n // b,),
        in_specs=[img(b, s.len, D), img(b, s.rows, 3 * D), img(b, s.rows, D), const(D, 3 * D), const(48, 128),
                  const(8, 8 * D + FF), const(8, 2 * D), const(z.r1, 128)],
        out_specs=[img(b, s.len, D), const(n, z.r0, 128)] + [const(*v) for v in shards],
        out_shape=[SDS(tokens.shape, F32), SDS((n, z.r0, 128), BF16)] + [SDS(v, F32) for v in shards],
        scratch_shapes=[VM((D, 3 * D), F32), VM((8, 2 * D), F32), VM((rows, D), BF16), VM((rows, D), BF16), VM((rows, 3 * D), BF16),
                        VM((3456 + 16, 128), F32), VM((48, 128), F32), VM((16, 128), F32)],
        compiler_params=big())(tokens, gt, gx, wqkv, sml, gsm, gqv, res)


def kernel5(n, part_in, res, part, rc, rb, s0, r0, local):
    place = Place(n)
    r = Reduce(place, part, rc, rb, s0, r0)
    copy = pltpu.make_async_copy(part_in, part, local)
    copy.start()
    greet(place)
    copy.wait()
    r.begin()
    for h, off in r.order():
        acc = r.advance(h, off)
        if not any(off):
            res[r.rows(h), :] = acc
    r.finish()


def call5(n, part):
    z, c = Sizes(n), n // 2
    return pl.pallas_call(
        functools.partial(kernel5, n), in_specs=[pl.BlockSpec(memory_space=pl.ANY)], out_specs=pl.BlockSpec(memory_space=VM),
        out_shape=SDS((z.r0, 128), F32),
        scratch_shapes=[VM((n, z.r0, 128), BF16), VM((c, z.r0, 128), BF16), VM((c, z.r0, 128), BF16)] + sems(n) + [pltpu.SemaphoreType.DMA],
        compiler_params=big(collective_id=2, has_side_effects=True))(part)


def kernel6(n, res, oq, on, ob):
    z = Sizes(n)
    oq[...] = res[:z.q, :]
    on[...] = res[z.small:z.small + 1, :z.norm]
    ob[...] = res[z.small + 1:z.small + 2, :z.bias]


def call6(n, res):
    z = Sizes(n)
    return pl.pallas_call(functools.partial(kernel6, n), out_shape=[SDS((z.q, 128), F32), SDS((1, z.norm), F32), SDS((1, z.bias), F32)])(res)


def local(n, tokens, cotangent, valid_slots, qkv_weight, out_weight, fc1_weight, fc2_weight, norm_params, bias_params):
    shards = [v.reshape(-1, 128) for v in (qkv_weight, out_weight, fc1_weight, fc2_weight)]
    shards += [norm_params.reshape(1, -1), bias_params.reshape(1, -1)]
    s = Pad(tokens)
    q, k, v, p, o, wqkv, wo, w1, w2, sml = call1(n, tokens, shards)
    out, gx, go, part1, gsm = call2(n, valid_slots, tokens, cotangent, o, wo, w1, w2, sml)
    gt, gqv, res1 = call3(n, s, q, k, v, p, go, part1)
    dx, part0, oo, o1, o2 = call4(n, tokens, gt, gx, wqkv, sml, gsm, gqv, res1)
    oq, on, ob = call6(n, call5(n, part0))
    return (out, dx) + tuple(v.reshape(-1) for v in (oq, oo, o1, o2, on, ob))


def solution(mesh):
    s3, s1 = P("dev", None, None), P("dev")
    return jax.shard_map(functools.partial(local, mesh.shape["dev"]), mesh=mesh, in_specs=(s3, s3) + (s1,) * 7,
                         out_specs=(s3, s3) + (s1,) * 6, check_vma=False)
```

time: 476 us -> 186 us (0.39)
  blocking collectives: 166 us -> 0 us
  waiting for transfers between devices: 123 us -> 0 us
  Pallas kernels: 132 us -> 185 us
  local copies, waits for them, and re-layouts: 32.4 us -> 0 us
  between operations: 13.8 us -> 0.67 us
  other arithmetic: 7.1 us -> 0 us
    unnamed x4 -> x0, waiting for transfers between devices: 123 us -> none
    all_gather x2 -> x0, blocking collectives: 84.5 us -> none  [local(): ag = lambda v: lax.all_gather(v, 'dev', axis=0, tiled=True)]
    unnamed x2 -> x0, blocking collectives: 81.7 us -> none
    pallas_call x1 -> x6, Pallas kernels: 132 us -> 185 us  [the longest x1 56.4 us: call2(): pl.pallas_call(functools.partial(kernel2, n, s, b, 256), grid_spec=grid_s...]
    reshape x11 -> x0, local copies, waits for them, and re-layouts: 21.2 us -> none  [the longest x1 3.47 us: local(): w1 = ag(fc1_weight).reshape(D, FF)]
    unnamed x16 -> x0, local copies, waits for them, and re-layouts: 11.3 us -> none
    all_gather x2 -> x0, other arithmetic: 7.05 us -> none  [local(): ag = lambda v: lax.all_gather(v, 'dev', axis=0, tiled=True)]
  transfers between devices with their start and end apart: 3 -> 0, of which waited for: 1 -> 0; matrix products, arithmetic and copies ran while one was open for 4% -> 0% of each run, Pallas kernels for 0% -> 0%
where the time goes in v2:
time: 186 us; the launch traced here: 185 us
  Pallas kernels  185 us (99%)
    pallas_call x1, Pallas kernels, call2(): pl.pallas_call(functools.partial(kernel2, n, s, b, 256), grid_spec=grid_s...  56.4 us
    pallas_call x1, Pallas kernels, call1(): pl.pallas_call(functools.partial(kernel1, n, s, b), grid=(s.n // b,), in_...  55 us
    pallas_call x1, Pallas kernels, call3(): pl.pallas_call(functools.partial(kernel3, n, s, b), grid=(s.n // b,), in_...  35.1 us
    pallas_call x1, Pallas kernels, call4(): pl.pallas_call(functools.partial(kernel4, n, s, b), grid=(s.n // b,), in_...  21.2 us
    pallas_call x1, Pallas kernels, call5(): pl.pallas_call(functools.partial(kernel5, n), in_specs=[pl.BlockSpec(memo...  15.6 us

profile of v2, /device:TPU:0, one launch (start us, length us, event | category | flops | bytes accessed | tf_op | source)
XLA Modules:
  0.0 185.3 jit_solution(8797744465185719190)
XLA Ops:
  0.6 55.0 %shard_map.152 = (bf16[18,256,384]{2,1,0:T(8,128)(2,1)}, bf16[18,208,384]{2,1,0:T(8,128)(2,1)}, bf16[18,208,384]{2,1,0:T(8,128)(2,1)}, bf16[18,3,208,512]{3,2,1,...) custom-call(bf16[18,197,384]{2,1,0:T(8,128)(2,1)} %x_ref.5, ...), custom_call_target="tpu_custom_call" | custom-call | tf_op jit(solution)/shard_map/pallas_call | solution.py:536
  55.6 56.4 %shard_map.153 = (bf16[18,197,384]{2,1,0:T(8,128)(2,1)}, f32[18,208,384]{2,1,0:T(8,128)}, bf16[18,256,384]{2,1,0:T(8,128)(2,1)}, bf16[32,352,128]{2,1,0:T(8,128)(2,1)}, f32[8,4608]{1,0:T(8,128)}) custom-call(s32[18]{0:T(128)} %valid.1, bf16[18,197,384]{2,1,0:T(8,128)(2,1)} %x_ref.5, bf16[18,197,384]{2,1,0:T(8,128)(2,1)} %c_ref.1, ...), custom_call_target="tpu_custom_call" | custom-call | tf_op jit(solution)/shard_map/pallas_call | solution.py:577
  112.0 35.1 %shard_map.154 = (bf16[18,208,1152]{2,1,0:T(8,128)(2,1)}, f32[8,768]{1,0:T(8,128)}, f32[352,128]{1,0:T(8,128)}) custom-call(bf16[18,256,384]{2,1,0:T(8,128)(2,1)} %get-tuple-element.40.q_ref, bf16[18,208,384]{2,1,0:T(8,128)(2,1)} %get-tuple-element.41.k_ref, bf16[18,208,384]{2,1,0:T(8,128)(2,1)} %get-tuple-element.42.v_ref, ...), custom_call_target="tpu_custom_call" | custom-call | tf_op jit(solution)/shard_map/pallas_call | solution.py:617
  147.2 21.2 %shard_map.155 = (f32[18,197,384]{2,1,0:T(8,128)}, bf16[32,128,128]{2,1,0:T(8,128)(2,1)}, f32[36,128]{1,0:T(8,128)}, f32[144,128]{1,0:T(8,128)}, f32[144,128]{1,0:T(8,128)}) custom-call(bf16[18,197,384]{2,1,0:T(8,128)(2,1)} %x_ref.5, bf16[18,208,1152]{2,1,0:T(8,128)(2,1)} %get-tuple-element.46.gt_ref, f32[18,208,384]{2,1,0:T(8,128)} %get-tuple-element.47.gx_ref, ...), custom_call_target="tpu_custom_call" | custom-call | tf_op jit(solution)/shard_map/pallas_call | solution.py:653
  168.3 15.6 %shard_map.156.res = f32[128,128]{1,0:T(8,128)} custom-call(bf16[32,128,128]{2,1,0:T(8,128)(2,1)} %get-tuple-element.53.part_in), custom_call_target="tpu_custom_call" | custom-call | tf_op jit(solution)/shard_map/pallas_call | solution.py:681
  183.9 1.5 shard_map.157

commit v3 on v2

v3 whole, which is shorter than its diff:
```python
import functools
import jax
import jax.numpy as jnp
from jax import lax
from jax.experimental import pallas as pl
from jax.experimental.pallas import tpu as pltpu
from jax.sharding import PartitionSpec as P

D, HEADS, HEAD_DIM, FF = 384, 6, 64, 1536
PAIRS = HEADS // 2
EPS = 1e-6
F32, BF16 = jnp.float32, jnp.bfloat16
RS2 = 0.7071067811865476
RS2PI = 0.3989422804014327
VM = pltpu.VMEM
BIAS_ROW = 16
SDS = jax.ShapeDtypeStruct


def nn(a, b):
    return lax.dot_general(a, b, (((1,), (0,)), ((), ())), preferred_element_type=F32)


def nt(a, b):
    return lax.dot_general(a, b, (((1,), (1,)), ((), ())), preferred_element_type=F32)


def tn(a, b):
    return lax.dot_general(a, b, (((0,), (0,)), ((), ())), preferred_element_type=F32)


def col8(v):
    return v.reshape(v.shape[0] // 8, 8, v.shape[1]).sum(axis=0)


def norm_fwd(v):
    c = v - jnp.mean(v, axis=1, keepdims=True)
    r = lax.rsqrt(jnp.mean(c * c, axis=1, keepdims=True) + EPS)
    return c * r, r


def norm_bwd(g, n, r, gain):
    e = g * gain
    return r * (e - jnp.mean(e, axis=1, keepdims=True) - n * jnp.mean(e * n, axis=1, keepdims=True))


def vec(sml, row, count=3):
    return jnp.concatenate([sml[row + j:row + j + 1, :] for j in range(count)], axis=1)


def low_lanes():
    return lax.broadcasted_iota(jnp.int32, (1, 128), 1) < 64


def stacked(v):
    low, z = low_lanes(), jnp.zeros_like(v)
    return jnp.concatenate([jnp.where(low, v, z), jnp.where(low, z, v)], axis=0)


class Pad:
    def __init__(self, tokens):
        self.n, self.len, _ = tokens.shape
        self.rows = -(-self.len // 16) * 16
        self.lanes = -(-self.len // 128) * 128

    def step(self, most):
        return max(b for b in range(1, most + 1) if self.n % b == 0)


def staged(items, *stages):
    held = {}
    for tick in range(len(items) + len(stages) - 1):
        for j in range(len(stages)):
            k = tick - j
            if 0 <= k < len(items):
                held[k] = stages[j](items[k], held.get(k))


def attn_fwd(s, b, h1, wqkv, sml, q_ref, k_ref, v_ref, p_ref, o_ref):
    lp, qp, low = s.rows, s.lanes, low_lanes()
    t = nn(h1[...], wqkv[...])
    q = (t[:, :D] + vec(sml, BIAS_ROW)).astype(BF16) * BF16(0.125)
    k = t[:, D:2 * D].astype(BF16)
    v = (t[:, 2 * D:] + vec(sml, BIAS_ROW + 3)).astype(BF16)
    for u in range(b):
        rows = slice(u * lp, u * lp + lp)
        q_ref[u, :lp, :] = q[rows]
        q_ref[u, lp:, :] = jnp.zeros((qp - lp, D), BF16)
        k_ref[u] = k[rows]
        v_ref[u] = v[rows]

    def scores(item, _):
        u, j = item
        cols = slice(128 * j, 128 * j + 128)
        return nt(k_ref[u, :, cols], stacked(q_ref[u, :, cols]))

    def softmax(item, st):
        u, j = item
        cols = slice(128 * j, 128 * j + 128)
        top, bot = st[:lp - 16], st[lp - 16:]
        row = lax.broadcasted_iota(jnp.int32, bot.shape, 0) + (lp - 16)
        bot = jnp.where(row < s.len, bot, -1e30)
        mx = jnp.maximum(jnp.max(top, axis=0, keepdims=True), jnp.max(bot, axis=0, keepdims=True))
        e = jnp.exp(jnp.concatenate([top, bot], axis=0) - mx)
        p = (e * (1.0 / jnp.sum(e, axis=0, keepdims=True))).astype(BF16)
        p_ref[u, j] = p

    def mix(item, _):
        u, j = item
        cols = slice(128 * j, 128 * j + 128)
        p, v = p_ref[u, j], v_ref[u, :, cols]
        o_ref[u, :, cols] = jnp.where(low, tn(p[:, :lp], v), tn(p[:, qp:qp + lp], v)).astype(BF16)

    staged([(u, j) for u in range(b) for j in range(PAIRS)], scores, softmax, mix)


def attn_bwd(s, b, q_ref, k_ref, v_ref, p_ref, go_ref, gt_ref, gts, gcs):
    lp, qp, low = s.rows, s.lanes, low_lanes()

    def first(item, _):
        u, j = item
        cols = slice(128 * j, 128 * j + 128)
        p, go = p_ref[u, j], go_ref[u, :, cols]
        gp = nt(v_ref[u, :, cols], stacked(go))
        gv = jnp.where(low, nn(p[:, :qp], go), nn(p[:, qp:], go))
        return gp, gv

    def middle(item, got):
        u, j = item
        gp, gv = got
        pf = p_ref[u, j].astype(F32)
        return (pf * (gp - jnp.sum(gp * pf, axis=0, keepdims=True))).astype(BF16), gv

    def rest(item, got):
        u, j = item
        gs, gv = got
        cols = slice(128 * j, 128 * j + 128)
        k, q = k_ref[u, :, cols], q_ref[u, :, cols]
        gq = jnp.where(low, tn(gs[:, :lp], k), tn(gs[:, qp:qp + lp], k)) * 0.125
        gk = jnp.where(low, nn(gs[:, :qp], q), nn(gs[:, qp:], q))
        for part, g in enumerate((gq, gk, gv)):
            here = slice(part * D + 128 * j, part * D + 128 * j + 128)
            gcs[:, here] += col8(g)
            g = g.astype(BF16)
            gt_ref[u, :, here] = g
            gts[u * lp:u * lp + lp, here] = g

    staged([(u, j) for u in range(b) for j in range(PAIRS)], first, middle, rest)


LOG2E = 1.4426950408889634
LOG2_2C = 0.17425193526384086
ROOT2 = 1.4142135623730951


def ffn(s, b, sb, ch, i, valid, x_ref, c_ref, o_ref, wo, w1x, w2, w2t, sml,
        out_ref, gx_ref, go_ref, gout, gfc1, gfc2t, gsm, xp, cp, ch_, os_, n2s, r2s, h2s, as_, gzs, x1s, gxb):
    lp, qp = s.rows, s.lanes
    g2, c2 = vec(sml, 6), vec(sml, 9)
    bo, b2 = vec(sml, BIAS_ROW + 6), vec(sml, BIAS_ROW + 21)
    sr = sb * lp
    rows_all = b * lp

    def sub(t, _):
        for u in range(sb):
            w = t * sb + u
            m = valid[i * b + w].astype(BF16)
            xp[u * lp:u * lp + s.len, :] = x_ref[w]
            r0 = pl.multiple_of(w * lp, lp)
            cp[pl.ds(r0, s.len), :] = c_ref[w] * m
            os_[pl.ds(r0, lp), :] = o_ref[w]
        rows = pl.ds(pl.multiple_of(t * sr, sr), sr)
        x1 = xp[...].astype(F32) + nn(os_[rows, :], wo[...]) + bo
        x1s[rows, :] = x1
        n2, r2 = norm_fwd(x1)
        n2s[rows, :] = n2
        r2s[rows, :] = r2
        h2s[rows, :D] = (n2 * g2 + c2).astype(BF16)
        ch_[...] = cp[rows, :] * BF16(0.5)
        for c in range(FF // ch):
            cols = slice(c * ch, (c + 1) * ch)
            z = nn(h2s[rows, :], w1x[:, cols])
            ga = nt(ch_[...], w2[cols, :])
            w = z * RS2
            u1 = 1.0 + lax.erf(w)
            as_[rows, cols] = (w * u1).astype(BF16)
            gzs[rows, cols] = (ga * (u1 + w * jnp.exp2(w * w * -LOG2E + LOG2_2C))).astype(BF16)
        return 0

    lax.fori_loop(0, b // sb, sub, 0)
    yt = nt(w2t[...], as_[...])
    gt = nt(w1x[:D, :], gzs[...])
    y = yt.T[:rows_all] * RS2 + x1s[...] + b2
    for u in range(b):
        out_ref[u] = (y[u * lp:u * lp + s.len] * valid[i * b + u].astype(F32)).astype(BF16)
    gh2 = gt.T[:rows_all]
    n2 = n2s[...]
    gy = cp[:rows_all, :].astype(F32)
    gsm[:, 2 * D:3 * D] += col8(gh2 * n2)
    gsm[:, 3 * D:4 * D] += col8(gh2)
    gsm[:, 7 * D + FF:] += col8(gy)
    gx1 = gy + norm_bwd(gh2, n2, r2s[...], g2)
    gsm[:, 6 * D:7 * D] += col8(gx1)
    gxb[:rows_all, :] = gx1.astype(BF16)
    gfc2t[...] += tn(cp[...], as_[...])
    gfc1[...] += tn(h2s[:, :D + 16], gzs[...])
    gout[...] += tn(os_[...], gxb[...])
    go = nt(gxb[:rows_all, :], wo[...]).astype(BF16)
    for u in range(b):
        gx_ref[u] = gx1[u * lp:u * lp + lp]
        go_ref[u, :lp, :] = go[u * lp:u * lp + lp]
        go_ref[u, lp:, :] = jnp.zeros((qp - lp, D), BF16)


def ffn_setup(s, b, w1, w2, sml, w1x, w2t, h2s):
    w1x[:D, :] = w1[...]
    w1x[D:D + 16, :] = jnp.concatenate([vec(sml, BIAS_ROW + 9, 12), jnp.zeros((15, FF), F32)], axis=0).astype(BF16)
    w1x[D + 16:, :] = jnp.zeros((112, FF), BF16)
    w2t[...] = w2[...].T
    lane = lax.broadcasted_iota(jnp.int32, (b * s.rows, 128), 1)
    h2s[:b * s.rows, D:] = jnp.where(lane == 0, 1.0, 0.0).astype(BF16)


def proj_bwd(s, b, x_ref, gt_ref, gx_ref, wqkv, sml, dx_ref, xp, gts):
    lp = s.rows
    for u in range(b):
        xp[u * lp:u * lp + s.len, :] = x_ref[u]
        gts[u * lp:u * lp + lp, :] = gt_ref[u]
    n1, r1 = norm_fwd(xp[...].astype(F32))
    back = norm_bwd(nt(gts[...], wqkv[...]), n1, r1, vec(sml, 0))
    for u in range(b):
        dx_ref[u] = gx_ref[u, :s.len] + back[u * lp:u * lp + s.len]


def zero(*refs):
    for r in refs:
        r[...] = jnp.zeros_like(r)


def img(b, *shape):
    return pl.BlockSpec((b,) + shape, lambda i, *_: (i,) + (0,) * len(shape))


def const(*shape):
    return pl.BlockSpec(shape, lambda i, *_: (0,) * len(shape), pipeline_mode=pl.Buffered(1))


def big(**kw):
    return pltpu.CompilerParams(vmem_limit_bytes=62 << 20, **kw)


MESHID = pl.DeviceIdType.MESH


def chip_dims(n):
    chips = n // 2
    side = 4 if chips >= 64 else 2
    return (chips // (side * side), side, side)


class Place:
    def __init__(self, n):
        self.n, self.dims = n, chip_dims(n)
        me = lax.axis_index("dev")
        self.me, self.core = me, lax.rem(me, 2)
        s0, s1, s2 = self.dims
        chip = me // 2
        self.at = (chip // (s1 * s2), lax.rem(chip // s2, s1), lax.rem(chip, s2))
        self.offs = [(a, b, c) for a in range(s0) for b in range(s1) for c in range(s2)]

    def chip(self, off):
        i0, i1, i2 = (lax.rem(i + s + o, s) for i, s, o in zip(self.at, self.dims, off))
        return (i0 * self.dims[1] + i1) * self.dims[2] + i2

    def dev(self, off):
        return 2 * self.chip(off) + self.core

    def partner(self, off=(0, 0, 0)):
        return 2 * self.chip(off) + 1 - self.core

    def num(self, off):
        return (off[0] * self.dims[1] + off[1]) * self.dims[2] + off[2]

    def peers(self):
        for k in range(3):
            for o in range(1, self.dims[k]):
                yield self.dev(unit(k, o))
        yield self.partner()


def unit(k, o):
    return tuple(o if j == k else 0 for j in range(3))


def neg(off):
    return tuple(-o for o in off)


def greet(pl_):
    barrier = pltpu.get_barrier_semaphore()
    count = 0
    for dev in pl_.peers():
        pl.semaphore_signal(barrier, inc=1, device_id=(dev,), device_id_type=MESHID)
        count += 1
    pl.semaphore_wait(barrier, count)


ORDERS = ((0, 2, 1), (0, 1, 2))


class Gather:
    def __init__(self, place, src, buf, ssem, rsem):
        self.p, self.src, self.buf, self.ssem, self.rsem = place, src, buf, ssem, rsem
        self.half = src.shape[0] // 2

    def link(self, h, off, to, dev):
        p, rows = self.p, pl.ds(h * self.half, self.half)
        origin = p.dev(neg(off))
        src = self.src.at[rows] if not any(off) else self.buf.at[origin, rows]
        k = p.num(to)
        return pltpu.make_async_remote_copy(
            src_ref=src, dst_ref=self.buf.at[origin, rows], send_sem=self.ssem.at[0, h, k],
            recv_sem=self.rsem.at[0, h, k], device_id=(dev,), device_id_type=MESHID)

    def cross(self, h, off):
        p, rows = self.p, pl.ds(h * self.half, self.half)
        origin = p.dev(neg(off))
        src = self.src.at[rows] if not any(off) else self.buf.at[origin, rows]
        k = p.num(off)
        return pltpu.make_async_remote_copy(
            src_ref=src, dst_ref=self.buf.at[origin, rows], send_sem=self.ssem.at[1, h, k],
            recv_sem=self.rsem.at[1, h, k], device_id=(p.partner(),), device_id_type=MESHID)

    def hops(self, h, off):
        order = ORDERS[h]
        last = max([j for j in range(3) if off[order[j]]], default=-1)
        for j in range(last + 1, 3):
            k = order[j]
            for o in range(1, self.p.dims[k]):
                to = tuple(a + b for a, b in zip(off, unit(k, o)))
                yield to, self.p.dev(unit(k, o))

    def forward(self, h, off):
        for to, dev in self.hops(h, off):
            self.link(h, off, to, dev).start()
        self.cross(h, off).start()

    def begin(self):
        for h in range(2):
            self.forward(h, (0, 0, 0))

    def arrivals(self):
        offs = sorted([o for o in self.p.offs if any(o)], key=lambda o: (sum(1 for a in o if a), min(o[0], self.p.dims[0] - o[0])))
        return [(h, o) for o in offs for h in range(2)]

    def arrive(self, h, off):
        self.link(h, off, off, self.p.me).wait_recv()
        self.forward(h, off)

    def finish(self):
        for h in range(2):
            for off in self.p.offs:
                c = self.cross(h, off)
                c.wait_recv()
                c.wait_send()
                for to, dev in self.hops(h, off):
                    self.link(h, off, to, dev).wait_send()


class Reduce:
    def __init__(self, place, part, rc, rb, ssem, rsem):
        self.p, self.part, self.rc, self.rb, self.ssem, self.rsem = place, part, rc, rb, ssem, rsem
        self.half = part.shape[1] // 2

    def rows(self, h):
        return pl.ds(h * self.half, self.half)

    def cross(self, h, off):
        p, k = self.p, self.p.num(off)
        return pltpu.make_async_remote_copy(
            src_ref=self.part.at[p.partner(off), self.rows(h)], dst_ref=self.rc.at[k, self.rows(h)],
            send_sem=self.ssem.at[1, h, k], recv_sem=self.rsem.at[1, h, k],
            device_id=(p.partner(),), device_id_type=MESHID)

    def step_dim(self, h, off):
        return [k for k in reversed(ORDERS[h]) if off[k]][0]

    def link(self, h, off):
        p, k = self.p, self.p.num(off)
        dim = self.step_dim(h, off)
        return pltpu.make_async_remote_copy(
            src_ref=self.part.at[p.dev(off), self.rows(h)], dst_ref=self.rb.at[k, self.rows(h)],
            send_sem=self.ssem.at[0, h, k], recv_sem=self.rsem.at[0, h, k],
            device_id=(p.dev(unit(dim, off[dim])),), device_id_type=MESHID)

    def sources(self, h, off):
        order = ORDERS[h]
        last = max([j for j in range(3) if off[order[j]]], default=-1)
        for j in reversed(range(last + 1, 3)):
            k = order[j]
            for o in range(1, self.p.dims[k]):
                yield tuple(a + b for a, b in zip(off, unit(k, o)))

    def order(self):
        offs = sorted(self.p.offs, key=lambda o: (-sum(1 for a in o if a), o))
        return [(h, o) for o in offs for h in range(2)]

    def begin(self):
        for h, off in self.order():
            self.cross(h, off).start()

    def total(self, h, off):
        p, k = self.p, self.p.num(off)
        self.cross(h, off).wait_recv()
        acc = self.part[p.dev(off), self.rows(h), :].astype(F32) + self.rc[k, self.rows(h), :].astype(F32)
        for s in self.sources(h, off):
            self.link(h, s).wait_recv()
            acc += self.rb[p.num(s), self.rows(h), :].astype(F32)
        return acc

    def advance(self, h, off):
        acc = self.total(h, off)
        if any(off):
            self.part[self.p.dev(off), self.rows(h), :] = acc.astype(BF16)
            self.link(h, off).start()
        return acc

    def finish(self):
        for h, off in self.order():
            self.cross(h, off).wait_send()
            if any(off):
                self.link(h, off).wait_send()


class Sizes:
    def __init__(self, n):
        up = lambda v, m: -(-v // m) * m
        self.n = n
        self.q, self.o, self.f = 3 * D * D // n // 128, D * D // n // 128, D * FF // n // 128
        self.norm, self.bias = 4 * D // n, (4 * D + FF) // n
        self.small = up(self.q, 16)
        self.r0 = up(self.small + 16, 32)
        self.f1 = up(self.o, 16)
        self.f2 = self.f1 + up(self.f, 16)
        self.r1 = up(self.f2 + up(self.f, 16), 32)


def sems(n):
    return [pltpu.SemaphoreType.DMA((2, 2, n // 2))] * 2


def levels(events):
    groups = {}
    for h, off in events:
        groups.setdefault(sum(1 for a in off if a), []).append((h, off))
    return groups


def at_step(i, k):
    return pl.when(i == k)


def unpack(z, buf, first, count, fl, w):
    def one(d, _):
        fl[pl.ds(d * count, count), :] = buf[d, first:first + -(-count // 16) * 16, :].astype(F32)[:count]
        return 0

    lax.fori_loop(0, z.n, one, 0)
    rows, cols = w.shape[0], w.shape[1] // 128
    for j in range(cols):
        w[:, 128 * j:128 * j + 128] = fl[pl.ds(j, rows, stride=cols), :].astype(BF16)


def unpack_small(z, buf, sml):
    lane = lax.broadcasted_iota(jnp.int32, (1, 128), 1)
    rows = {}

    def put(v, start, size):
        first, shift = divmod(start, 128)
        v = pltpu.roll(v, shift, axis=1) if shift else v
        cut = (lane >= shift) & (lane < shift + size)
        rows[first] = jnp.where(cut, v, rows.get(first, 0.0))
        if shift + size > 128:
            rows[first + 1] = jnp.where(lane < shift + size - 128, v, rows.get(first + 1, 0.0))

    for d in range(z.n):
        v = buf[d, z.small:z.small + 16, :].astype(F32)
        put(v[0:1], d * z.norm, z.norm)
        put(v[1:2], BIAS_ROW * 128 + d * z.bias, z.bias)
    for r, v in rows.items():
        sml[r:r + 1, :] = v


def flatten(g, rows, fl):
    cols = g.shape[1] // 128
    for j in range(cols):
        fl[pl.ds(j, rows, stride=cols), :] = g[:rows, 128 * j:128 * j + 128]


def pack(z, fl, count, first, part):
    size = -(-count // 16) * 16

    def one(d, _):
        part[d, first:first + size, :] = fl[pl.ds(d * count, size), :].astype(BF16)
        return 0

    lax.fori_loop(0, z.n, one, 0)


def column(row):
    return jnp.broadcast_to(row, (128, 128)).T


def finish_qkv(z, nacc, gcs, wqkv, sml, gsm, fl, part):
    total = jnp.sum(gcs[...], axis=0, keepdims=True)
    gain, shift = vec(sml, 0), vec(sml, 3)
    rows = {}
    for a in range(3):
        ra = slice(128 * a, 128 * a + 128)
        g, c = column(gain[:, ra]), column(shift[:, ra])
        q1, q2 = jnp.zeros((128, 128), F32), jnp.zeros((128, 128), F32)
        for j in range(9):
            cols = slice(128 * j, 128 * j + 128)
            na, w = nacc[ra, cols], wqkv[ra, cols].astype(F32)
            fl[pl.ds(9 * 128 * a + j, 128, stride=9), :] = g * na + c * total[:, cols]
            q1 += w * na
            q2 += w * total[:, cols]
        rows[a] = jnp.sum(q1.T, axis=0, keepdims=True)
        rows[3 + a] = jnp.sum(q2.T, axis=0, keepdims=True)
        rows[BIAS_ROW + a] = total[:, 128 * a:128 * a + 128]
        rows[BIAS_ROW + 3 + a] = total[:, 2 * D + 128 * a:2 * D + 128 * a + 128]

    def put(first, count, base):
        v = jnp.sum(gsm[:, first:first + 128 * count], axis=0, keepdims=True)
        for j in range(count):
            rows[base + j] = v[:, 128 * j:128 * j + 128]

    put(2 * D, 6, 6)
    put(6 * D, 18, BIAS_ROW + 6)
    pack(z, fl, z.q, 0, part)
    lane = lax.broadcasted_iota(jnp.int32, (1, 128), 1)

    def take(start, size):
        first, shift = divmod(start, 128)
        v = rows[first]
        if shift + size > 128:
            v = jnp.where(lane >= shift, v, rows[first + 1])
        return pltpu.roll(v, 128 - shift, axis=1) if shift else v

    for d in range(z.n):
        both = [take(d * z.norm, z.norm), take(BIAS_ROW * 128 + d * z.bias, z.bias)]
        part[d, z.small:z.small + 16, :] = jnp.concatenate(both + [jnp.zeros((14, 128), F32)], axis=0).astype(BF16)


def kernel1(n, s, b, x_hbm, q_in, o_in, f1_in, f2_in, n_in, b_in, q_ref, k_ref, v_ref, p_ref, o_ref, n_ref,
            wqkv, wo, w1, w2, sml, tok, n1s, h1, x0, x1, buf0, buf1, fl, st, s0, r0, s1, r1, local):
    i, last = pl.program_id(0), s.n // b - 1
    z = Sizes(n)
    place = Place(n)
    a, c = Gather(place, x0, buf0, s0, r0), Gather(place, x1, buf1, s1, r1)

    def norms(first, past):
        def one(u, _):
            r = pl.multiple_of(u * s.rows, s.rows)
            n1s[pl.ds(r + s.rows - 16, 16), :] = jnp.zeros((16, D), F32)
            n1s[pl.ds(r, s.len), :] = norm_fwd(tok[u].astype(F32))[0]
            return 0

        lax.fori_loop(first, past, one, 0)

    @pl.when(i == 0)
    def _():
        copy = pltpu.make_async_copy(x_hbm, tok, local)
        copy.start()
        zero(sml, st, x0, x1)
        st[0:1, :z.norm] = n_in[...].astype(F32)
        st[1:2, :z.bias] = b_in[...].astype(F32)
        x0[:z.q, :] = q_in[...]
        x0[z.small:z.small + 16, :] = st[:16, :].astype(BF16)
        x1[:z.o, :] = o_in[...]
        x1[z.f1:z.f1 + z.f, :] = f1_in[...]
        x1[z.f2:z.f2 + z.f, :] = f2_in[...]
        buf0[place.me] = x0[...]
        buf1[place.me] = x1[...]
        greet(place)
        a.begin()
        copy.wait()
        groups = levels(a.arrivals())
        for k, level in enumerate(groups):
            norms(k * s.n // len(groups), (k + 1) * s.n // len(groups))
            for h, off in groups[level]:
                a.arrive(h, off)
        a.finish()
        c.begin()
        unpack_small(z, buf0, sml)
        unpack(z, buf0, 0, z.q, fl, wqkv)

    rows = b * s.rows
    n1 = n1s[pl.ds(pl.multiple_of(i * rows, rows), rows), :]
    h1[...] = (n1 * vec(sml, 0) + vec(sml, 3)).astype(BF16)
    for u in range(b):
        n_ref[u] = n1[u * s.rows:(u + 1) * s.rows].astype(BF16)
    attn_fwd(s, b, h1, wqkv, sml, q_ref, k_ref, v_ref, p_ref, o_ref)

    for level, events in levels(c.arrivals()).items():
        @pl.when(i == min(2 * level, last))
        def _():
            for h, off in events:
                c.arrive(h, off)

    @pl.when(i == last)
    def _():
        c.finish()
        unpack(z, buf1, 0, z.o, fl, wo)
        unpack(z, buf1, z.f1, z.f, fl, w1)
        unpack(z, buf1, z.f2, z.f, fl, w2)


def call1(n, tokens, shards):
    s, z = Pad(tokens), Sizes(n)
    b = s.step(2)
    saved = [((s.lanes, D), BF16), ((s.rows, D), BF16), ((s.rows, D), BF16), ((PAIRS, s.rows, 2 * s.lanes), BF16), ((s.rows, D), BF16), ((s.rows, D), BF16)]
    whole = [((D, 3 * D), BF16), ((D, D), BF16), ((D, FF), BF16), ((FF, D), BF16), ((48, 128), F32)]
    return pl.pallas_call(
        functools.partial(kernel1, n, s, b), grid=(s.n // b,),
        in_specs=[pl.BlockSpec(memory_space=pl.ANY)] + [const(*v.shape) for v in shards],
        out_specs=[img(b, *v[0]) for v in saved] + [const(*v[0]) for v in whole],
        out_shape=[SDS((s.n,) + v[0], v[1]) for v in saved] + [SDS(*v) for v in whole],
        scratch_shapes=[VM((s.n, s.len, D), BF16), VM((s.n * s.rows, D), F32), VM((b * s.rows, D), BF16),
                        VM((z.r0, 128), BF16), VM((z.r1, 128), BF16), VM((n, z.r0, 128), BF16), VM((n, z.r1, 128), BF16),
                        VM((4608 + 16, 128), F32), VM((16, 128), F32)] + sems(n) + sems(n) + [pltpu.SemaphoreType.DMA],
        compiler_params=big(collective_id=0, has_side_effects=True))(tokens, *shards)


def kernel2(n, s, b, sb, ch, valid, x_ref, c_ref, o_ref, wo, w1, w2, sml, out_ref, gx_ref, go_ref, part, gsm,
            xp, cp, ch_, os_, n2s, r2s, h2s, as_, gzs, x1s, gxb, w1x, w2t, gout, gfc1, gfc2t, fl):
    i = pl.program_id(0)
    z = Sizes(n)
    rows = b * s.rows

    @pl.when(i == 0)
    def _():
        zero(xp, cp, gout, gfc1, gfc2t, gsm)
        for r in (os_, h2s, as_, gzs, gxb):
            pad = r.shape[0] - rows
            if pad:
                r[rows:, :] = jnp.zeros((pad, r.shape[1]), BF16)
        ffn_setup(s, b, w1, w2, sml, w1x, w2t, h2s)

    ffn(s, b, sb, ch, i, valid, x_ref, c_ref, o_ref, wo, w1x, w2, w2t, sml, out_ref, gx_ref, go_ref,
        gout, gfc1, gfc2t, gsm, xp, cp, ch_, os_, n2s, r2s, h2s, as_, gzs, x1s, gxb)

    @pl.when(i == s.n // b - 1)
    def _():
        zero(part)
        gsm[0:1, 7 * D:7 * D + FF] = gfc1[D:D + 1, :]
        flatten(gout, D, fl)
        pack(z, fl, z.o, 0, part)
        flatten(gfc1, D, fl)
        pack(z, fl, z.f, z.f1, part)
        for j in range(3):
            fl[pl.ds(j, FF, stride=3), :] = gfc2t[128 * j:128 * j + 128, :].T * RS2
        pack(z, fl, z.f, z.f2, part)


def call2(n, valid, tokens, cot, o, wo, w1, w2, sml):
    s, z = Pad(tokens), Sizes(n)
    b = s.step(6)
    sb = max(k for k in range(1, 4) if b % k == 0)
    rows = b * s.rows
    up, sr = -(-rows // 256) * 256, sb * s.rows
    grid_spec = pltpu.PrefetchScalarGridSpec(
        num_scalar_prefetch=1, grid=(s.n // b,),
        in_specs=[img(b, s.len, D), img(b, s.len, D), img(b, s.rows, D), const(D, D), const(D, FF), const(FF, D), const(48, 128)],
        out_specs=[img(b, s.len, D), img(b, s.rows, D), img(b, s.lanes, D), const(n, z.r1, 128), const(8, 8 * D + FF)],
        scratch_shapes=[VM((sr, D), BF16), VM((up, D), BF16), VM((sr, D), BF16), VM((up, D), BF16), VM((rows, D), F32), VM((rows, 1), F32),
                        VM((up, D + 128), BF16), VM((up, FF), BF16), VM((up, FF), BF16), VM((rows, D), F32), VM((up, D), BF16),
                        VM((D + 128, FF), BF16), VM((D, FF), BF16), VM((D, D), F32), VM((D + 16, FF), F32), VM((D, FF), F32),
                        VM((4608 + 16, 128), F32)])
    return pl.pallas_call(
        functools.partial(kernel2, n, s, b, sb, 256), grid_spec=grid_spec,
        out_shape=[SDS(tokens.shape, BF16), SDS((s.n, s.rows, D), F32), SDS((s.n, s.lanes, D), BF16),
                   SDS((n, z.r1, 128), BF16), SDS((8, 8 * D + FF), F32)],
        compiler_params=big())(valid, tokens, cot, o, wo, w1, w2, sml)


def kernel3(n, s, b, q_ref, k_ref, v_ref, p_ref, go_ref, n_ref, wqkv, sml, gsm, part_in, gt_ref, part0, res,
            part, rc, rb, nacc, gcs, n1b, gts, fl, s1, r1, local):
    i, last = pl.program_id(0), s.n // b - 1
    z = Sizes(n)
    place = Place(n)
    r = Reduce(place, part, rc, rb, s1, r1)

    @pl.when(i == 0)
    def _():
        copy = pltpu.make_async_copy(part_in, part, local)
        copy.start()
        zero(nacc, gcs)
        greet(place)
        copy.wait()
        r.begin()

    attn_bwd(s, b, q_ref, k_ref, v_ref, p_ref, go_ref, gt_ref, gts, gcs)
    for u in range(b):
        n1b[u * s.rows:(u + 1) * s.rows, :] = n_ref[u]
    nacc[...] += tn(n1b[...], gts[...])

    @pl.when(i == last)
    def _():
        zero(part0)
        finish_qkv(z, nacc, gcs, wqkv, sml, gsm, fl, part0)

    for level, events in levels(r.order()).items():
        @pl.when(i == min(2 + 2 * (3 - level), last))
        def _():
            for h, off in events:
                acc = r.advance(h, off)
                if not any(off):
                    res[r.rows(h), :] = acc

    @pl.when(i == last)
    def _():
        r.finish()


def call3(n, s, q, k, v, p, go, n1, wqkv, sml, gsm, part):
    z = Sizes(n)
    b = s.step(2)
    c, rows = n // 2, b * s.rows
    return pl.pallas_call(
        functools.partial(kernel3, n, s, b), grid=(s.n // b,),
        in_specs=[img(b, s.lanes, D), img(b, s.rows, D), img(b, s.rows, D), img(b, PAIRS, s.rows, 2 * s.lanes), img(b, s.lanes, D),
                  img(b, s.rows, D), const(D, 3 * D), const(48, 128), const(8, 8 * D + FF), pl.BlockSpec(memory_space=pl.ANY)],
        out_specs=[img(b, s.rows, 3 * D), const(n, z.r0, 128), const(z.r1, 128)],
        out_shape=[SDS((s.n, s.rows, 3 * D), BF16), SDS((n, z.r0, 128), BF16), SDS((z.r1, 128), F32)],
        scratch_shapes=[VM((n, z.r1, 128), BF16), VM((c, z.r1, 128), BF16), VM((c, z.r1, 128), BF16),
                        VM((D, 3 * D), F32), VM((8, 3 * D), F32), VM((rows, D), BF16), VM((rows, 3 * D), BF16),
                        VM((3456 + 16, 128), F32)] + sems(n) + [pltpu.SemaphoreType.DMA],
        compiler_params=big(collective_id=1, has_side_effects=True))(q, k, v, p, go, n1, wqkv, sml, gsm, part)


def kernel4(n, s, b, x_ref, gt_ref, gx_ref, wqkv, sml, part_in, dx_ref, res, part, rc, rb, xp, gts, s0, r0, local):
    i, last = pl.program_id(0), s.n // b - 1
    place = Place(n)
    r = Reduce(place, part, rc, rb, s0, r0)

    @pl.when(i == 0)
    def _():
        copy = pltpu.make_async_copy(part_in, part, local)
        copy.start()
        zero(xp)
        greet(place)
        copy.wait()
        r.begin()

    proj_bwd(s, b, x_ref, gt_ref, gx_ref, wqkv, sml, dx_ref, xp, gts)

    for level, events in levels(r.order()).items():
        @pl.when(i == min(1 + 2 * (3 - level), last))
        def _():
            for h, off in events:
                acc = r.advance(h, off)
                if not any(off):
                    res[r.rows(h), :] = acc

    @pl.when(i == last)
    def _():
        r.finish()


def call4(n, tokens, gt, gx, wqkv, sml, part):
    s, z = Pad(tokens), Sizes(n)
    b = s.step(2)
    c, rows = n // 2, b * s.rows
    return pl.pallas_call(
        functools.partial(kernel4, n, s, b), grid=(s.n // b,),
        in_specs=[img(b, s.len, D), img(b, s.rows, 3 * D), img(b, s.rows, D), const(D, 3 * D), const(48, 128), pl.BlockSpec(memory_space=pl.ANY)],
        out_specs=[img(b, s.len, D), const(z.r0, 128)],
        out_shape=[SDS(tokens.shape, F32), SDS((z.r0, 128), F32)],
        scratch_shapes=[VM((n, z.r0, 128), BF16), VM((c, z.r0, 128), BF16), VM((c, z.r0, 128), BF16),
                        VM((rows, D), BF16), VM((rows, 3 * D), BF16)] + sems(n) + [pltpu.SemaphoreType.DMA],
        compiler_params=big(collective_id=2, has_side_effects=True))(tokens, gt, gx, wqkv, sml, part)


def kernel5(n, dx_in, res0, res1, dx, oq, oo, o1, o2, on, ob):
    z = Sizes(n)
    dx[...] = dx_in[...]

    @pl.when(pl.program_id(0) == 0)
    def _():
        oq[...] = res0[:z.q, :]
        on[...] = res0[z.small:z.small + 1, :z.norm]
        ob[...] = res0[z.small + 1:z.small + 2, :z.bias]
        oo[...] = res1[:z.o, :]
        o1[...] = res1[z.f1:z.f1 + z.f, :]
        o2[...] = res1[z.f2:z.f2 + z.f, :]


def call5(n, dx, res0, res1):
    s, z = Pad(dx), Sizes(n)
    b = s.step(3)
    shapes = [(z.q, 128), (z.o, 128), (z.f, 128), (z.f, 128), (1, z.norm), (1, z.bias)]
    return pl.pallas_call(
        functools.partial(kernel5, n), grid=(s.n // b,),
        in_specs=[img(b, s.len, D), const(z.r0, 128), const(z.r1, 128)],
        out_specs=[img(b, s.len, D)] + [const(*v) for v in shapes],
        out_shape=[SDS(dx.shape, F32)] + [SDS(v, F32) for v in shapes],
        compiler_params=big())(dx, res0, res1)


def local(n, tokens, cotangent, valid_slots, qkv_weight, out_weight, fc1_weight, fc2_weight, norm_params, bias_params):
    shards = [v.reshape(-1, 128) for v in (qkv_weight, out_weight, fc1_weight, fc2_weight)]
    shards += [norm_params.reshape(1, -1), bias_params.reshape(1, -1)]
    s = Pad(tokens)
    q, k, v, p, o, n1, wqkv, wo, w1, w2, sml = call1(n, tokens, shards)
    out, gx, go, part1, gsm = call2(n, valid_slots, tokens, cotangent, o, wo, w1, w2, sml)
    gt, part0, res1 = call3(n, s, q, k, v, p, go, n1, wqkv, sml, gsm, part1)
    dx, res0 = call4(n, tokens, gt, gx, wqkv, sml, part0)
    dx, *grads = call5(n, dx, res0, res1)
    return (out, dx) + tuple(v.reshape(-1) for v in grads)


def solution(mesh):
    s3, s1 = P("dev", None, None), P("dev")
    return jax.shard_map(functools.partial(local, mesh.shape["dev"]), mesh=mesh, in_specs=(s3, s3) + (s1,) * 7,
                         out_specs=(s3, s3) + (s1,) * 6, check_vma=False)
```

time: 186 us -> 162 us (0.87)
  Pallas kernels: 185 us -> 161 us
    pallas_call x3 -> x2, Pallas kernels: 73.4 us -> 58.8 us  [the longest x1 52.2 us: call2(): pl.pallas_call(functools.partial(kernel2, n, s, b, sb, 256), grid_spec=gr...]
    pallas_call x1, Pallas kernels: 55 us -> 48.8 us  [call1(): pl.pallas_call(functools.partial(kernel1, n, s, b), grid=(s.n // b,), in_...]
    pallas_call x1, Pallas kernels: 21.2 us -> 19.1 us  [call4(): pl.pallas_call(functools.partial(kernel4, n, s, b), grid=(s.n // b,), in_...]
where the time goes in v3:
time: 162 us; the launch traced here: 161 us
  Pallas kernels  161 us (99%)
    pallas_call x1, Pallas kernels, call2(): pl.pallas_call(functools.partial(kernel2, n, s, b, sb, 256), grid_spec=gr...  52.2 us
    pallas_call x1, Pallas kernels, call1(): pl.pallas_call(functools.partial(kernel1, n, s, b), grid=(s.n // b,), in_...  48.8 us
    pallas_call x1, Pallas kernels, call3(): pl.pallas_call(functools.partial(kernel3, n, s, b), grid=(s.n // b,), in_...  33.9 us
    pallas_call x1, Pallas kernels, call4(): pl.pallas_call(functools.partial(kernel4, n, s, b), grid=(s.n // b,), in_...  19.1 us
    pallas_call x1, Pallas kernels, call5(): pl.pallas_call(functools.partial(kernel5, n), grid=(s.n // b,), in_specs=...  6.56 us

profile of v3, /device:TPU:0, one launch (start us, length us, event | category | flops | bytes accessed | tf_op | source)
XLA Modules:
  0.0 161.4 jit_solution(4683894348409367913)
XLA Ops:
  0.6 48.8 %shard_map.152 = (bf16[18,256,384]{2,1,0:T(8,128)(2,1)}, bf16[18,208,384]{2,1,0:T(8,128)(2,1)}, bf16[18,208,384]{2,1,0:T(8,128)(2,1)}, bf16[18,3,208,512]{3,2,1,...) custom-call(bf16[18,197,384]{2,1,0:T(8,128)(2,1)} %x_ref.3, ...), custom_call_target="tpu_custom_call" | custom-call | tf_op jit(solution)/shard_map/pallas_call | solution.py:624
  49.4 52.2 %shard_map.153 = (bf16[18,197,384]{2,1,0:T(8,128)(2,1)}, f32[18,208,384]{2,1,0:T(8,128)}, bf16[18,256,384]{2,1,0:T(8,128)(2,1)}, bf16[32,352,128]{2,1,0:T(8,128)(2,1)}, f32[8,4608]{1,0:T(8,128)}) custom-call(s32[18]{0:T(128)} %valid.1, bf16[18,197,384]{2,1,0:T(8,128)(2,1)} %x_ref.3, bf16[18,197,384]{2,1,0:T(8,128)(2,1)} %c_ref.1, ...), custom_call_target="tpu_custom_call" | custom-call | tf_op jit(solution)/shard_map/pallas_call | solution.py:680
  101.7 33.9 %shard_map.154 = (bf16[18,208,1152]{2,1,0:T(8,128)(2,1)}, bf16[32,128,128]{2,1,0:T(8,128)(2,1)}, f32[352,128]{1,0:T(8,128)}) custom-call(bf16[18,256,384]{2,1,0:T(8,128)(2,1)} %get-tuple-element.42.q_ref, bf16[18,208,384]{2,1,0:T(8,128)(2,1)} %get-tuple-element.43.k_ref, bf16[18,208,384]{2,1,0:T(8,128)(2,1)} %get-tuple-element.44.v_ref, ...), custom_call_target="tpu_custom_call" | custom-call | tf_op jit(solution)/shard_map/pallas_call | solution.py:730
  135.5 19.1 %shard_map.155 = (f32[18,197,384]{2,1,0:T(8,128)}, f32[128,128]{1,0:T(8,128)}) custom-call(bf16[18,197,384]{2,1,0:T(8,128)(2,1)} %x_ref.3, bf16[18,208,1152]{2,1,0:T(8,128)(2,1)} %get-tuple-element.51.gt_ref, f32[18,208,384]{2,1,0:T(8,128)} %get-tuple-element.52.gx_ref, bf16[384,1152]{1,0:T(8,128)(2,1)} %get-tuple-element.48.wqkv, ...), custom_call_target="tpu_custom_call" | custom-call | tf_op jit(solution)/shard_map/pallas_call | solution.py:775
  154.6 6.6 %shard_map.156 = (f32[18,197,384]{2,1,0:T(8,128)}, f32[108,128]{1,0:T(8,128)}, f32[36,128]{1,0:T(8,128)}, f32[144,128]{1,0:T(8,128)}, f32[144,128]{1,0:T(8,128)}, /*index=5*/f32[1,48]{1,0:T(1,128)}, f32[1,96]{1,0:T(1,128)}) custom-call(f32[18,197,384]{2,1,0:T(8,128)} %get-tuple-element.54.dx_in, f32[128,128]{1,0:T(8,128)} %get-tuple-element.55.res0, ...), custom_call_target="tpu_custom_call" | custom-call | tf_op jit(solution)/shard_map/pallas_call | solution.py:803

commit v4 on v3

--- a/solution.py
+++ b/solution.py
@@ -207,7 +207,7 @@
     gout[...] += tn(os_[...], gxb[...])
     go = nt(gxb[:rows_all, :], wo[...]).astype(BF16)
     for u in range(b):
-        gx_ref[u] = gx1[u * lp:u * lp + lp]
+        gx_ref[u] = gxb[u * lp:u * lp + lp, :]
         go_ref[u, :lp, :] = go[u * lp:u * lp + lp]
         go_ref[u, lp:, :] = jnp.zeros((qp - lp, D), BF16)
 
@@ -229,7 +229,7 @@
     n1, r1 = norm_fwd(xp[...].astype(F32))
     back = norm_bwd(nt(gts[...], wqkv[...]), n1, r1, vec(sml, 0))
     for u in range(b):
-        dx_ref[u] = gx_ref[u, :s.len] + back[u * lp:u * lp + s.len]
+        dx_ref[u] = (gx_ref[u].astype(F32) + back[u * lp:u * lp + lp]).astype(BF16)[:s.len]
 
 
 def zero(*refs):
@@ -679,7 +679,7 @@
                         VM((4608 + 16, 128), F32)])
     return pl.pallas_call(
         functools.partial(kernel2, n, s, b, sb, 256), grid_spec=grid_spec,
-        out_shape=[SDS(tokens.shape, BF16), SDS((s.n, s.rows, D), F32), SDS((s.n, s.lanes, D), BF16),
+        out_shape=[SDS(tokens.shape, BF16), SDS((s.n, s.rows, D), BF16), SDS((s.n, s.lanes, D), BF16),
                    SDS((n, z.r1, 128), BF16), SDS((8, 8 * D + FF), F32)],
         compiler_params=big())(valid, tokens, cot, o, wo, w1, w2, sml)
 
@@ -776,7 +776,7 @@
         functools.partial(kernel4, n, s, b), grid=(s.n // b,),
         in_specs=[img(b, s.len, D), img(b, s.rows, 3 * D), img(b, s.rows, D), const(D, 3 * D), const(48, 128), pl.BlockSpec(memory_space=pl.ANY)],
         out_specs=[img(b, s.len, D), const(z.r0, 128)],
-        out_shape=[SDS(tokens.shape, F32), SDS((z.r0, 128), F32)],
+        out_shape=[SDS(tokens.shape, BF16), SDS((z.r0, 128), F32)],
         scratch_shapes=[VM((n, z.r0, 128), BF16), VM((c, z.r0, 128), BF16), VM((c, z.r0, 128), BF16),
                         VM((rows, D), BF16), VM((rows, 3 * D), BF16)] + sems(n) + [pltpu.SemaphoreType.DMA],
         compiler_params=big(collective_id=2, has_side_effects=True))(tokens, gt, gx, wqkv, sml, part)
@@ -784,7 +784,7 @@
 
 def kernel5(n, dx_in, res0, res1, dx, oq, oo, o1, o2, on, ob):
     z = Sizes(n)
-    dx[...] = dx_in[...]
+    dx[...] = dx_in[...].astype(F32)
 
     @pl.when(pl.program_id(0) == 0)
     def _():

time: 162 us -> 161 us (level)
  Pallas kernels: 161 us -> 159 us
where the time goes in v4:
time: 161 us; the launch traced here: 160 us
  Pallas kernels  159 us (99%)
    pallas_call x1, Pallas kernels, call2(): pl.pallas_call(functools.partial(kernel2, n, s, b, sb, 256), grid_spec=gr...  52.3 us
    pallas_call x1, Pallas kernels, call1(): pl.pallas_call(functools.partial(kernel1, n, s, b), grid=(s.n // b,), in_...  48.8 us
    pallas_call x1, Pallas kernels, call3(): pl.pallas_call(functools.partial(kernel3, n, s, b), grid=(s.n // b,), in_...  33.9 us
    pallas_call x1, Pallas kernels, call4(): pl.pallas_call(functools.partial(kernel4, n, s, b), grid=(s.n // b,), in_...  18.6 us
    pallas_call x1, Pallas kernels, call5(): pl.pallas_call(functools.partial(kernel5, n), grid=(s.n // b,), in_specs=...  5.69 us

profile of v4, /device:TPU:0, one launch (start us, length us, event | category | flops | bytes accessed | tf_op | source)
XLA Modules:
  0.0 160.1 jit_solution(14561213742833769822)
XLA Ops:
  0.6 48.8 %shard_map.152 = (bf16[18,256,384]{2,1,0:T(8,128)(2,1)}, bf16[18,208,384]{2,1,0:T(8,128)(2,1)}, bf16[18,208,384]{2,1,0:T(8,128)(2,1)}, bf16[18,3,208,512]{3,2,1,...) custom-call(bf16[18,197,384]{2,1,0:T(8,128)(2,1)} %x_ref.3, ...), custom_call_target="tpu_custom_call" | custom-call | tf_op jit(solution)/shard_map/pallas_call | solution.py:624
  49.4 52.3 %shard_map.153 = (bf16[18,197,384]{2,1,0:T(8,128)(2,1)}, bf16[18,208,384]{2,1,0:T(8,128)(2,1)}, bf16[18,256,384]{2,1,0:T(8,128)(2,1)}, bf16[32,352,128]{2,1,0:T(8,128)(2,1)}, f32[8,4608]{1,0:T(8,128)}) custom-call(s32[18]{0:T(128)} %valid.1, bf16[18,197,384]{2,1,0:T(8,128)(2,1)} %x_ref.3, bf16[18,197,384]{2,1,0:T(8,128)(2,1)} %c_ref.1, ...), custom_call_target="tpu_custom_call" | custom-call | tf_op jit(solution)/shard_map/pallas_call | solution.py:680
  101.7 33.9 %shard_map.154 = (bf16[18,208,1152]{2,1,0:T(8,128)(2,1)}, bf16[32,128,128]{2,1,0:T(8,128)(2,1)}, f32[352,128]{1,0:T(8,128)}) custom-call(bf16[18,256,384]{2,1,0:T(8,128)(2,1)} %get-tuple-element.42.q_ref, bf16[18,208,384]{2,1,0:T(8,128)(2,1)} %get-tuple-element.43.k_ref, bf16[18,208,384]{2,1,0:T(8,128)(2,1)} %get-tuple-element.44.v_ref, ...), custom_call_target="tpu_custom_call" | custom-call | tf_op jit(solution)/shard_map/pallas_call | solution.py:730
  135.7 18.6 %shard_map.155 = (bf16[18,197,384]{2,1,0:T(8,128)(2,1)}, f32[128,128]{1,0:T(8,128)}) custom-call(bf16[18,197,384]{2,1,0:T(8,128)(2,1)} %x_ref.3, bf16[18,208,1152]{2,1,0:T(8,128)(2,1)} %get-tuple-element.51.gt_ref, bf16[18,208,384]{2,1,0:T(8,128)(2,1)} %get-tuple-element.52.gx_ref, bf16[384,1152]{1,0:T(8,128)(2,1)} %get-tuple-element.48.wqkv, ...), custom_call_target="tpu_custom_call" | custom-call | tf_op jit(solution)/shard_map/pallas_call | solution.py:775
  154.2 5.7 %shard_map.156 = (f32[18,197,384]{2,1,0:T(8,128)}, f32[108,128]{1,0:T(8,128)}, f32[36,128]{1,0:T(8,128)}, f32[144,128]{1,0:T(8,128)}, f32[144,128]{1,0:T(8,128)}, /*index=5*/f32[1,48]{1,0:T(1,128)}, f32[1,96]{1,0:T(1,128)}) custom-call(bf16[18,197,384]{2,1,0:T(8,128)(2,1)} %get-tuple-element.54.dx_in, f32[128,128]{1,0:T(8,128)} %get-tuple-element.55.res0, ...), custom_call_target="tpu_custom_call" | custom-call | tf_op jit(solution)/shard_map/pallas_call | solution.py:803

commit v5 on v4

--- a/solution.py
+++ b/solution.py
@@ -261,22 +261,26 @@
 class Place:
     def __init__(self, n):
         self.n, self.dims = n, chip_dims(n)
-        me = lax.axis_index("dev")
-        self.me, self.core = me, lax.rem(me, 2)
         s0, s1, s2 = self.dims
-        chip = me // 2
-        self.at = (chip // (s1 * s2), lax.rem(chip // s2, s1), lax.rem(chip, s2))
+        self.me = lax.axis_index("dev")
+        self.core = lax.rem(self.me, 2)
+        chip = self.me // 2
+        at = (chip // (s1 * s2), lax.rem(chip // s2, s1), lax.rem(chip, s2))
+        pitch = (2 * s1 * s2, 2 * s2, 2)
+        self.term = [[(lax.rem(i + o, s) if o else i) * w for o in range(s)] for i, s, w in zip(at, self.dims, pitch)]
         self.offs = [(a, b, c) for a in range(s0) for b in range(s1) for c in range(s2)]
-
-    def chip(self, off):
-        i0, i1, i2 = (lax.rem(i + s + o, s) for i, s, o in zip(self.at, self.dims, off))
-        return (i0 * self.dims[1] + i1) * self.dims[2] + i2
+        base = {o: self.term[0][o[0]] + self.term[1][o[1]] + self.term[2][o[2]] for o in self.offs}
+        self.same = {o: v + self.core for o, v in base.items()}
+        self.other = {o: v + 1 - self.core for o, v in base.items()}
+
+    def key(self, off):
+        return tuple(o % s for o, s in zip(off, self.dims))
 
     def dev(self, off):
-        return 2 * self.chip(off) + self.core
+        return self.same[self.key(off)]
 
     def partner(self, off=(0, 0, 0)):
-        return 2 * self.chip(off) + 1 - self.core
+        return self.other[self.key(off)]
 
     def num(self, off):
         return (off[0] * self.dims[1] + off[1]) * self.dims[2] + off[2]
@@ -306,6 +310,10 @@
 
 
 ORDERS = ((0, 2, 1), (0, 1, 2))
+
+
+def stage(h, off):
+    return max([j for j in range(3) if off[ORDERS[h][j]]], default=-1)
 
 
 class Gather:
@@ -346,8 +354,21 @@
         self.cross(h, off).start()
 
     def begin(self):
+        self.begin_first()
+        self.begin_rest()
+
+    def begin_first(self):
         for h in range(2):
-            self.forward(h, (0, 0, 0))
+            for to, dev in self.hops(h, (0, 0, 0)):
+                if to[ORDERS[h][0]]:
+                    self.link(h, (0, 0, 0), to, dev).start()
+
+    def begin_rest(self):
+        for h in range(2):
+            for to, dev in self.hops(h, (0, 0, 0)):
+                if not to[ORDERS[h][0]]:
+                    self.link(h, (0, 0, 0), to, dev).start()
+            self.cross(h, (0, 0, 0)).start()
 
     def arrivals(self):
         offs = sorted([o for o in self.p.offs if any(o)], key=lambda o: (sum(1 for a in o if a), min(o[0], self.p.dims[0] - o[0])))
@@ -368,7 +389,8 @@
 
 
 class Reduce:
-    def __init__(self, place, part, rc, rb, ssem, rsem):
+    def __init__(self, place, part, rc, rb, ssem, rsem, key):
+        self.key = key
         self.p, self.part, self.rc, self.rb, self.ssem, self.rsem = place, part, rc, rb, ssem, rsem
         self.half = part.shape[1] // 2
 
@@ -402,18 +424,19 @@
                 yield tuple(a + b for a, b in zip(off, unit(k, o)))
 
     def order(self):
-        offs = sorted(self.p.offs, key=lambda o: (-sum(1 for a in o if a), o))
-        return [(h, o) for o in offs for h in range(2)]
+        return sorted([(h, o) for o in self.p.offs for h in range(2)], key=lambda e: (-self.key(*e), e[1]))
 
     def begin(self):
         for h, off in self.order():
             self.cross(h, off).start()
 
-    def total(self, h, off):
+    def total(self, h, off, first=0):
         p, k = self.p, self.p.num(off)
         self.cross(h, off).wait_recv()
         acc = self.part[p.dev(off), self.rows(h), :].astype(F32) + self.rc[k, self.rows(h), :].astype(F32)
         for s in self.sources(h, off):
+            if stage(h, s) < first:
+                continue
             self.link(h, s).wait_recv()
             acc += self.rb[p.num(s), self.rows(h), :].astype(F32)
         return acc
@@ -425,10 +448,10 @@
             self.link(h, off).start()
         return acc
 
-    def finish(self):
+    def finish(self, first=0):
         for h, off in self.order():
             self.cross(h, off).wait_send()
-            if any(off):
+            if stage(h, off) >= first:
                 self.link(h, off).wait_send()
 
 
@@ -449,11 +472,20 @@
     return [pltpu.SemaphoreType.DMA((2, 2, n // 2))] * 2
 
 
-def levels(events):
+def count(h, off):
+    return sum(1 for a in off if a)
+
+
+def groups_by(key, events):
     groups = {}
     for h, off in events:
-        groups.setdefault(sum(1 for a in off if a), []).append((h, off))
+        groups.setdefault(key(h, off), []).append((h, off))
     return groups
+
+
+AT_GATHER = {1: 2, 2: 5}
+AT_FIRST = {2: 2, 1: 5}
+AT_SECOND = {3: 1, 2: 3, 1: 5, 0: 7}
 
 
 def at_step(i, k):
@@ -584,16 +616,19 @@
         buf1[place.me] = x1[...]
         greet(place)
         a.begin()
+        c.begin_first()
         copy.wait()
-        groups = levels(a.arrivals())
+        groups = groups_by(count, a.arrivals())
         for k, level in enumerate(groups):
             norms(k * s.n // len(groups), (k + 1) * s.n // len(groups))
             for h, off in groups[level]:
                 a.arrive(h, off)
         a.finish()
-        c.begin()
+        c.begin_rest()
         unpack_small(z, buf0, sml)
         unpack(z, buf0, 0, z.q, fl, wqkv)
+        for h, off in groups_by(stage, c.arrivals())[0]:
+            c.arrive(h, off)
 
     rows = b * s.rows
     n1 = n1s[pl.ds(pl.multiple_of(i * rows, rows), rows), :]
@@ -602,8 +637,10 @@
         n_ref[u] = n1[u * s.rows:(u + 1) * s.rows].astype(BF16)
     attn_fwd(s, b, h1, wqkv, sml, q_ref, k_ref, v_ref, p_ref, o_ref)
 
-    for level, events in levels(c.arrivals()).items():
-        @pl.when(i == min(2 * level, last))
+    for leg in (1, 2):
+        events = groups_by(stage, c.arrivals())[leg]
+
+        @pl.when(i == min(AT_GATHER[leg], last))
         def _():
             for h, off in events:
                 c.arrive(h, off)
@@ -684,12 +721,12 @@
         compiler_params=big())(valid, tokens, cot, o, wo, w1, w2, sml)
 
 
-def kernel3(n, s, b, q_ref, k_ref, v_ref, p_ref, go_ref, n_ref, wqkv, sml, gsm, part_in, gt_ref, part0, res,
+def kernel3(n, s, b, q_ref, k_ref, v_ref, p_ref, go_ref, n_ref, wqkv, sml, gsm, part_in, gt_ref, part0, mid,
             part, rc, rb, nacc, gcs, n1b, gts, fl, s1, r1, local):
     i, last = pl.program_id(0), s.n // b - 1
     z = Sizes(n)
     place = Place(n)
-    r = Reduce(place, part, rc, rb, s1, r1)
+    r = Reduce(place, part, rc, rb, s1, r1, stage)
 
     @pl.when(i == 0)
     def _():
@@ -710,17 +747,18 @@
         zero(part0)
         finish_qkv(z, nacc, gcs, wqkv, sml, gsm, fl, part0)
 
-    for level, events in levels(r.order()).items():
-        @pl.when(i == min(2 + 2 * (3 - level), last))
+    legs = groups_by(stage, r.order())
+    for leg in (2, 1):
+        @pl.when(i == min(AT_FIRST[leg], last))
         def _():
-            for h, off in events:
-                acc = r.advance(h, off)
-                if not any(off):
-                    res[r.rows(h), :] = acc
+            for h, off in legs[leg]:
+                r.advance(h, off)
 
     @pl.when(i == last)
     def _():
-        r.finish()
+        for h, off in legs[0] + legs[-1]:
+            mid[off[0], r.rows(h), :] = r.total(h, off, 1).astype(BF16)
+        r.finish(1)
 
 
 def call3(n, s, q, k, v, p, go, n1, wqkv, sml, gsm, part):
@@ -731,32 +769,43 @@
         functools.partial(kernel3, n, s, b), grid=(s.n // b,),
         in_specs=[img(b, s.lanes, D), img(b, s.rows, D), img(b, s.rows, D), img(b, PAIRS, s.rows, 2 * s.lanes), img(b, s.lanes, D),
                   img(b, s.rows, D), const(D, 3 * D), const(48, 128), const(8, 8 * D + FF), pl.BlockSpec(memory_space=pl.ANY)],
-        out_specs=[img(b, s.rows, 3 * D), const(n, z.r0, 128), const(z.r1, 128)],
-        out_shape=[SDS((s.n, s.rows, 3 * D), BF16), SDS((n, z.r0, 128), BF16), SDS((z.r1, 128), F32)],
+        out_specs=[img(b, s.rows, 3 * D), const(n, z.r0, 128), const(chip_dims(n)[0], z.r1, 128)],
+        out_shape=[SDS((s.n, s.rows, 3 * D), BF16), SDS((n, z.r0, 128), BF16), SDS((chip_dims(n)[0], z.r1, 128), BF16)],
         scratch_shapes=[VM((n, z.r1, 128), BF16), VM((c, z.r1, 128), BF16), VM((c, z.r1, 128), BF16),
                         VM((D, 3 * D), F32), VM((8, 3 * D), F32), VM((rows, D), BF16), VM((rows, 3 * D), BF16),
                         VM((3456 + 16, 128), F32)] + sems(n) + [pltpu.SemaphoreType.DMA],
         compiler_params=big(collective_id=1, has_side_effects=True))(q, k, v, p, go, n1, wqkv, sml, gsm, part)
 
 
-def kernel4(n, s, b, x_ref, gt_ref, gx_ref, wqkv, sml, part_in, dx_ref, res, part, rc, rb, xp, gts, s0, r0, local):
+def kernel4(n, s, b, x_ref, gt_ref, gx_ref, wqkv, sml, part_in, mid_in, dx_ref, res, res1,
+            part, rc, rb, mid, rz, xp, gts, s0, r0, sz, qz, local):
     i, last = pl.program_id(0), s.n // b - 1
     place = Place(n)
-    r = Reduce(place, part, rc, rb, s0, r0)
+    r = Reduce(place, part, rc, rb, s0, r0, count)
+    far = range(1, place.dims[0])
+
+    def along(o):
+        return pltpu.make_async_remote_copy(
+            src_ref=mid.at[o], dst_ref=rz.at[o], send_sem=sz.at[o], recv_sem=qz.at[o],
+            device_id=(place.dev((o, 0, 0)),), device_id_type=MESHID)
 
     @pl.when(i == 0)
     def _():
-        copy = pltpu.make_async_copy(part_in, part, local)
-        copy.start()
+        copies = [pltpu.make_async_copy(part_in, part, local.at[0]), pltpu.make_async_copy(mid_in, mid, local.at[1])]
+        for copy in copies:
+            copy.start()
         zero(xp)
         greet(place)
-        copy.wait()
+        for copy in copies:
+            copy.wait()
         r.begin()
+        for o in far:
+            along(o).start()
 
     proj_bwd(s, b, x_ref, gt_ref, gx_ref, wqkv, sml, dx_ref, xp, gts)
 
-    for level, events in levels(r.order()).items():
-        @pl.when(i == min(1 + 2 * (3 - level), last))
+    for level, events in groups_by(count, r.order()).items():
+        @pl.when(i == min(AT_SECOND[level], last))
         def _():
             for h, off in events:
                 acc = r.advance(h, off)
@@ -765,21 +814,30 @@
 
     @pl.when(i == last)
     def _():
+        acc = mid[0].astype(F32)
+        for o in far:
+            along(o).wait_recv()
+            acc += rz[o].astype(F32)
+        res1[...] = acc
+        for o in far:
+            along(o).wait_send()
         r.finish()
 
 
-def call4(n, tokens, gt, gx, wqkv, sml, part):
+def call4(n, tokens, gt, gx, wqkv, sml, part, mid):
     s, z = Pad(tokens), Sizes(n)
     b = s.step(2)
     c, rows = n // 2, b * s.rows
     return pl.pallas_call(
         functools.partial(kernel4, n, s, b), grid=(s.n // b,),
-        in_specs=[img(b, s.len, D), img(b, s.rows, 3 * D), img(b, s.rows, D), const(D, 3 * D), const(48, 128), pl.BlockSpec(memory_space=pl.ANY)],
-        out_specs=[img(b, s.len, D), const(z.r0, 128)],
-        out_shape=[SDS(tokens.shape, BF16), SDS((z.r0, 128), F32)],
+        in_specs=[img(b, s.len, D), img(b, s.rows, 3 * D), img(b, s.rows, D), const(D, 3 * D), const(48, 128)] + [pl.BlockSpec(memory_space=pl.ANY)] * 2,
+        out_specs=[img(b, s.len, D), const(z.r0, 128), const(z.r1, 128)],
+        out_shape=[SDS(tokens.shape, BF16), SDS((z.r0, 128), F32), SDS((z.r1, 128), F32)],
         scratch_shapes=[VM((n, z.r0, 128), BF16), VM((c, z.r0, 128), BF16), VM((c, z.r0, 128), BF16),
-                        VM((rows, D), BF16), VM((rows, 3 * D), BF16)] + sems(n) + [pltpu.SemaphoreType.DMA],
-        compiler_params=big(collective_id=2, has_side_effects=True))(tokens, gt, gx, wqkv, sml, part)
+                        VM(mid.shape, BF16), VM(mid.shape, BF16),
+                        VM((rows, D), BF16), VM((rows, 3 * D), BF16)] + sems(n)
+                       + [pltpu.SemaphoreType.DMA(mid.shape[:1])] * 2 + [pltpu.SemaphoreType.DMA((2,))],
+        compiler_params=big(collective_id=2, has_side_effects=True))(tokens, gt, gx, wqkv, sml, part, mid)
 
 
 def kernel5(n, dx_in, res0, res1, dx, oq, oo, o1, o2, on, ob):
@@ -814,8 +872,8 @@
     s = Pad(tokens)
     q, k, v, p, o, n1, wqkv, wo, w1, w2, sml = call1(n, tokens, shards)
     out, gx, go, part1, gsm = call2(n, valid_slots, tokens, cotangent, o, wo, w1, w2, sml)
-    gt, part0, res1 = call3(n, s, q, k, v, p, go, n1, wqkv, sml, gsm, part1)
-    dx, res0 = call4(n, tokens, gt, gx, wqkv, sml, part0)
+    gt, part0, mid = call3(n, s, q, k, v, p, go, n1, wqkv, sml, gsm, part1)
+    dx, res0, res1 = call4(n, tokens, gt, gx, wqkv, sml, part0, mid)
     dx, *grads = call5(n, dx, res0, res1)
     return (out, dx) + tuple(v.reshape(-1) for v in grads)
 

time: 161 us -> 160 us (level)
  no operation moved by 1% of the time
where the time goes in v5:
time: 160 us; the launch traced here: 159 us
  Pallas kernels  159 us (99%)
    pallas_call x1, Pallas kernels, call2(): pl.pallas_call(functools.partial(kernel2, n, s, b, sb, 256), grid_spec=gr...  52.3 us
    pallas_call x1, Pallas kernels, call1(): pl.pallas_call(functools.partial(kernel1, n, s, b), grid=(s.n // b,), in_...  48.5 us
    pallas_call x1, Pallas kernels, call3(): pl.pallas_call(functools.partial(kernel3, n, s, b), grid=(s.n // b,), in_...  32.9 us
    pallas_call x1, Pallas kernels, call4(): pl.pallas_call(functools.partial(kernel4, n, s, b), grid=(s.n // b,), in_...  19.3 us
    pallas_call x1, Pallas kernels, call5(): pl.pallas_call(functools.partial(kernel5, n), grid=(s.n // b,), in_specs=...  5.69 us

profile of v5, /device:TPU:0, one launch (start us, length us, event | category | flops | bytes accessed | tf_op | source)
XLA Modules:
  0.0 159.5 jit_solution(12991390004063154362)
XLA Ops:
  0.6 48.5 %shard_map.152 = (bf16[18,256,384]{2,1,0:T(8,128)(2,1)}, bf16[18,208,384]{2,1,0:T(8,128)(2,1)}, bf16[18,208,384]{2,1,0:T(8,128)(2,1)}, bf16[18,3,208,512]{3,2,1,...) custom-call(bf16[18,197,384]{2,1,0:T(8,128)(2,1)} %x_ref.3, ...), custom_call_target="tpu_custom_call" | custom-call | tf_op jit(solution)/shard_map/pallas_call | solution.py:661
  49.1 52.3 %shard_map.153 = (bf16[18,197,384]{2,1,0:T(8,128)(2,1)}, bf16[18,208,384]{2,1,0:T(8,128)(2,1)}, bf16[18,256,384]{2,1,0:T(8,128)(2,1)}, bf16[32,352,128]{2,1,0:T(8,128)(2,1)}, f32[8,4608]{1,0:T(8,128)}) custom-call(s32[18]{0:T(128)} %valid.1, bf16[18,197,384]{2,1,0:T(8,128)(2,1)} %x_ref.3, bf16[18,197,384]{2,1,0:T(8,128)(2,1)} %c_ref.1, ...), custom_call_target="tpu_custom_call" | custom-call | tf_op jit(solution)/shard_map/pallas_call | solution.py:717
  101.4 32.9 %shard_map.154 = (bf16[18,208,1152]{2,1,0:T(8,128)(2,1)}, bf16[32,128,128]{2,1,0:T(8,128)(2,1)}, bf16[4,352,128]{2,1,0:T(8,128)(2,1)}) custom-call(bf16[18,256,384]{2,1,0:T(8,128)(2,1)} %get-tuple-element.43.q_ref, bf16[18,208,384]{2,1,0:T(8,128)(2,1)} %get-tuple-element.44.k_ref, bf16[18,208,384]{2,1,0:T(8,128)(2,1)} %get-tuple-element.45.v_ref, ...), custom_call_target="tpu_custom_call" | custom-call | tf_op jit(solution)/shard_map/pallas_call | solution.py:768
  134.3 19.3 %shard_map.155 = (bf16[18,197,384]{2,1,0:T(8,128)(2,1)}, f32[128,128]{1,0:T(8,128)}, f32[352,128]{1,0:T(8,128)}) custom-call(bf16[18,197,384]{2,1,0:T(8,128)(2,1)} %x_ref.3, bf16[18,208,1152]{2,1,0:T(8,128)(2,1)} %get-tuple-element.52.gt_ref, bf16[18,208,384]{2,1,0:T(8,128)(2,1)} %get-tuple-element.53.gx_ref, bf16[384,1152]{1,0:T(8,128)(2,1)} %get-tuple-element.49.wqkv, ...), custom_call_target="tpu_custom_call" | custom-call | tf_op jit(solution)/shard_map/pallas_call | solution.py:831
  153.6 5.7 %shard_map.156 = (f32[18,197,384]{2,1,0:T(8,128)}, f32[108,128]{1,0:T(8,128)}, f32[36,128]{1,0:T(8,128)}, f32[144,128]{1,0:T(8,128)}, f32[144,128]{1,0:T(8,128)}, /*index=5*/f32[1,48]{1,0:T(1,128)}, f32[1,96]{1,0:T(1,128)}) custom-call(bf16[18,197,384]{2,1,0:T(8,128)(2,1)} %get-tuple-element.56.dx_in, f32[128,128]{1,0:T(8,128)} %get-tuple-element.57.res0, ...), custom_call_target="tpu_custom_call" | custom-call | tf_op jit(solution)/shard_map/pallas_call | solution.py:861
